TPU v7x, 32 devices: a whole 2x2x4 slice. The times are simulated.
32 devices in a mesh: dp: 4 (over y, x), rows: 2 (over core), cols: 4 (over z).
Axes of the slice: x: 2, y: 2, z: 4, core: 2. Of those that a mesh axis runs over, the one named last changes fastest.
Arguments:
- tokens: bfloat16 [4, 2, 1024, 768], P(None, 'rows', 'dp', 'cols'), may hold values from -6 to 6
- cotangent: bfloat16 [4, 2, 1024, 768], P(None, 'rows', 'dp', 'cols'), may hold values from -6 to 6
- labels: int32 [4, 2], P(None, 'rows'), may hold values from 0 to 13
- q_weight: bfloat16 [768, 768], P('rows', 'cols'), may hold values from -0.3125 to 0.3125
- k_weight: bfloat16 [768, 768], P('rows', 'cols'), may hold values from -0.3125 to 0.3125
- v_weight: bfloat16 [768, 768], P('rows', 'cols'), may hold values from -0.21875 to 0.21875
- out_weight: bfloat16 [768, 768], P('cols', 'rows'), may hold values from -2.5 to 2.5
- up_weight: bfloat16 [768, 3072], P('rows', 'cols'), may hold values from -0.21875 to 0.21875
- down_weight: bfloat16 [3072, 768], P('cols', 'rows'), may hold values from -0.109375 to 0.109375
- ln1_gain: float32 [768], P('cols'), may hold values from 0.5 to 1.5
- ln1_bias: float32 [768], P('cols'), may hold values from -3 to 3
- ln2_gain: float32 [768], P('cols'), may hold values from 0.5 to 1.5
- ln2_bias: float32 [768], P('cols'), may hold values from -3 to 3
- cls_in: bfloat16 [768, 128], P('cols'), may hold values from -0.21875 to 0.21875
- pool_query: float32 [2, 64], replicated, may hold values from -8 to 8
- cls_mid: float32 [128, 128], replicated, may hold values from -0.5 to 0.5
- cls_out: float32 [128, 14], replicated, may hold values from -1.5 to 1.5
Outputs:
- out_y: bfloat16 [4, 2, 1024, 768], P(None, 'rows', 'dp', 'cols')
- losses: float32 [4, 2], P(None, 'rows')
- grad_tokens: float32 [4, 2, 1024, 768], P(None, 'rows', 'dp', 'cols')
- grad_q_weight: float32 [768, 768], P('rows', 'cols')
- grad_k_weight: float32 [768, 768], P('rows', 'cols')
- grad_v_weight: float32 [768, 768], P('rows', 'cols')
- grad_out_weight: float32 [768, 768], P('cols', 'rows')
- grad_up_weight: float32 [768, 3072], P('rows', 'cols')
- grad_down_weight: float32 [3072, 768], P('cols', 'rows')
- grad_ln1_gain: float32 [768], P('cols')
- grad_ln1_bias: float32 [768], P('cols')
- grad_ln2_gain: float32 [768], P('cols')
- grad_ln2_bias: float32 [768], P('cols')
- grad_cls_in: float32 [768, 128], P('cols')
- grad_pool_query: float32 [2, 64], replicated
- grad_cls_mid: float32 [128, 128], replicated
- grad_cls_out: float32 [128, 14], replicated
All inputs are finite; a program needn't handle non-finite values.
Results may differ from a plain program's by a relative error of at most 0.034.
Values may be sent and summed in bfloat16 or wider, within the bound.
A program may use at most 192 MiB of HBM per device.

v0:
```python
import math

import jax
import jax.numpy as jnp
from jax import lax
from jax.sharding import PartitionSpec as P

D = 768
HDIM = 64
CLS_D = 128
POOL_HEADS = 2
CLASSES = 14


eps_norm = 1e-12
highest = lax.Precision.HIGHEST


def merged(part, axis, combine):
    gathered = jax.tree.map(lambda a: lax.all_gather(a, axis), part)

    def take(source):
        return jax.tree.map(lambda a: lax.dynamic_index_in_dim(a, source, 0, False), gathered)

    return lax.fori_loop(
        1, lax.axis_size(axis), lambda source, state: combine(state, take(source)), take(0)
    )


def features(shard_part):
    return lax.all_gather(shard_part, "cols", axis=1, tiled=True)


def spread_sum(partial_value):
    return lax.psum_scatter(
        partial_value.astype(jnp.bfloat16), "cols", scatter_dimension=1, tiled=True
    ).astype(jnp.float32)


def token_sums(plain_sum, cross_sum):
    return lax.psum((plain_sum, cross_sum), "cols")


def dot_rows(left_mat, right_mat):
    return lax.dot_general(
        left_mat, right_mat, (((0,), (0,)), ((), ())), preferred_element_type=jnp.float32
    )


def dot_cols(left_mat, right_mat):
    return lax.dot_general(
        left_mat, right_mat, (((1,), (1,)), ((), ())), preferred_element_type=jnp.float32
    )


def exact_gelu(values):
    return jax.nn.gelu(values, approximate=False)


def norm_forward(hidden, gain_vec, shift_vec):
    plain_sum, squares = token_sums(jnp.sum(hidden, axis=1), jnp.sum(hidden * hidden, axis=1))
    average = plain_sum / D
    inv_std = lax.rsqrt(squares / D - average * average + eps_norm)
    centred = (hidden - average[:, None]) * inv_std[:, None]
    return (centred * gain_vec + shift_vec, centred, inv_std)


def norm_backward(upstream, centred, inv_std, gain_vec):
    scaled = upstream * gain_vec
    plain_sum, cross_sum = token_sums(jnp.sum(scaled, axis=1), jnp.sum(scaled * centred, axis=1))
    return inv_std[:, None] * (
        scaled - (plain_sum / D)[:, None] - centred * (cross_sum / D)[:, None]
    )


def block_size(number):
    return max((divisor for divisor in range(1, min(number, 1024) + 1) if number % divisor == 0))


def head_scores(query_heads, key_heads):
    return jnp.einsum(
        "qhd,khd->hqk", query_heads, key_heads, preferred_element_type=jnp.float32
    ) * (1.0 / math.sqrt(HDIM))


def split_pair(key_block, head_cols):
    block_rows = key_block.shape[0]
    key_heads = key_block[:, :head_cols].reshape(block_rows, head_cols // HDIM, HDIM)
    value_heads = key_block[:, head_cols:].reshape(block_rows, head_cols // HDIM, HDIM)
    return (key_heads, value_heads)


def fold_keys(running, shard_piece, query_heads):
    head_cols = query_heads.shape[1] * HDIM
    number = shard_piece.shape[0]
    block_rows = block_size(number)

    def fold_one_block(state_now, block_index):
        row_top, row_total, weighted = state_now
        key_block = lax.dynamic_slice_in_dim(shard_piece, block_index * block_rows, block_rows, 0)
        key_heads, value_heads = split_pair(key_block, head_cols)
        scores = head_scores(query_heads, key_heads)
        new_top = jnp.maximum(row_top, jnp.max(scores, axis=2))
        exp_scores = jnp.exp(scores - new_top[:, :, None])
        factor = jnp.exp(row_top - new_top)
        row_total = row_total * factor + jnp.sum(exp_scores, axis=2)
        weighted = weighted * jnp.transpose(factor)[:, :, None] + jnp.einsum(
            "hqk,khd->qhd",
            exp_scores.astype(jnp.bfloat16),
            value_heads,
            preferred_element_type=jnp.float32,
        )
        return ((new_top, row_total, weighted), None)

    running, unused = lax.scan(fold_one_block, running, jnp.arange(number // block_rows))
    return running


def score_grads(query_heads, key_heads, value_heads, grad_heads, log_total, delta_rows):
    softmaxed = jnp.exp(head_scores(query_heads, key_heads) - log_total[:, :, None])
    dprobs = jnp.einsum("qhd,khd->hqk", grad_heads, value_heads, preferred_element_type=jnp.float32)
    return (softmaxed, (softmaxed * (dprobs - delta_rows[:, :, None])).astype(jnp.bfloat16))


def joint_grads(pair_all, query_heads, grad_heads, log_total, delta_rows):
    head_cols = query_heads.shape[1] * HDIM
    number = pair_all.shape[0]
    block_rows = block_size(number)
    inv_root = 1.0 / math.sqrt(HDIM)

    def joint_one_block(accum, block_index):
        key_block = lax.dynamic_slice_in_dim(pair_all, block_index * block_rows, block_rows, 0)
        key_heads, value_heads = split_pair(key_block, head_cols)
        softmaxed, dscores = score_grads(
            query_heads, key_heads, value_heads, grad_heads, log_total, delta_rows
        )
        accum = accum + jnp.einsum(
            "hqk,khd->qhd", dscores, key_heads, preferred_element_type=jnp.float32
        )
        dkeys_block = (
            jnp.einsum("hqk,qhd->khd", dscores, query_heads, preferred_element_type=jnp.float32)
            * inv_root
        )
        dvalues = jnp.einsum(
            "hqk,qhd->khd",
            softmaxed.astype(jnp.bfloat16),
            grad_heads,
            preferred_element_type=jnp.float32,
        )
        return (
            accum,
            jnp.concatenate(
                [
                    dkeys_block.reshape(block_rows, head_cols),
                    dvalues.reshape(block_rows, head_cols),
                ],
                axis=1,
            ),
        )

    accum, blocks = lax.scan(
        joint_one_block, jnp.zeros(query_heads.shape, jnp.float32), jnp.arange(number // block_rows)
    )
    return (accum * inv_root, blocks.reshape(number, 2 * head_cols))


def pool_combine(left_part, right_part):
    top_left, total_left, sum_left = left_part
    top_right, total_right, sum_right = right_part
    joint_top = jnp.maximum(top_left, top_right)
    scale_left = jnp.exp(top_left - joint_top)
    scale_right = jnp.exp(top_right - joint_top)
    return (
        joint_top,
        total_left * scale_left + total_right * scale_right,
        sum_left * scale_left[:, None] + sum_right * scale_right[:, None],
    )


def reduce_weights(grad_set, head_cols):
    grad_qkv, grad_attn_out, grad_up, grad_down = grad_set
    part_q, part_k, part_v, part_out, part_up, part_down = (
        lax.psum_scatter(
            grad_qkv[:, :head_cols].astype(jnp.bfloat16), "rows", scatter_dimension=0, tiled=True
        ).astype(jnp.float32),
        lax.psum_scatter(
            grad_qkv[:, head_cols : 2 * head_cols].astype(jnp.bfloat16),
            "rows",
            scatter_dimension=0,
            tiled=True,
        ).astype(jnp.float32),
        lax.psum_scatter(
            grad_qkv[:, 2 * head_cols :].astype(jnp.bfloat16),
            "rows",
            scatter_dimension=0,
            tiled=True,
        ).astype(jnp.float32),
        lax.psum_scatter(
            grad_attn_out.astype(jnp.bfloat16), "rows", scatter_dimension=1, tiled=True
        ).astype(jnp.float32),
        lax.psum_scatter(
            grad_up.astype(jnp.bfloat16), "rows", scatter_dimension=0, tiled=True
        ).astype(jnp.float32),
        lax.psum_scatter(
            grad_down.astype(jnp.bfloat16), "rows", scatter_dimension=1, tiled=True
        ).astype(jnp.float32),
    )
    return (
        lax.psum(part_q.astype(jnp.bfloat16), "dp").astype(jnp.float32),
        lax.psum(part_k.astype(jnp.bfloat16), "dp").astype(jnp.float32),
        lax.psum(part_v.astype(jnp.bfloat16), "dp").astype(jnp.float32),
        lax.psum(part_out.astype(jnp.bfloat16), "dp").astype(jnp.float32),
        lax.psum(part_up.astype(jnp.bfloat16), "dp").astype(jnp.float32),
        lax.psum(part_down.astype(jnp.bfloat16), "dp").astype(jnp.float32),
    )


def body(
    tokens,
    cotangent,
    labels,
    q_weight,
    k_weight,
    v_weight,
    out_weight,
    up_weight,
    down_weight,
    ln1_gain,
    ln1_bias,
    ln2_gain,
    ln2_bias,
    cls_in,
    pool_query,
    cls_mid,
    cls_out,
):
    q_full, k_full, v_full, out_full, up_full, down_full = (
        lax.all_gather(q_weight, "rows", axis=0, tiled=True),
        lax.all_gather(k_weight, "rows", axis=0, tiled=True),
        lax.all_gather(v_weight, "rows", axis=0, tiled=True),
        lax.all_gather(out_weight, "rows", axis=1, tiled=True),
        lax.all_gather(up_weight, "rows", axis=0, tiled=True),
        lax.all_gather(down_weight, "rows", axis=1, tiled=True),
    )
    qkv_full = jnp.concatenate([q_full, k_full, v_full], axis=1)
    head_cols = q_weight.shape[1]
    heads_here = head_cols // HDIM
    row_count = tokens.shape[2]
    pool_dim = CLS_D // POOL_HEADS
    pool_root = math.sqrt(pool_dim)
    local_grads = (
        jnp.zeros(qkv_full.shape, jnp.float32),
        jnp.zeros(out_full.shape, jnp.float32),
        jnp.zeros(up_full.shape, jnp.float32),
        jnp.zeros(down_full.shape, jnp.float32),
    )
    gain_one = jnp.zeros(ln1_gain.shape, jnp.float32)
    bias_one = jnp.zeros(ln1_gain.shape, jnp.float32)
    gain_two = jnp.zeros(ln1_gain.shape, jnp.float32)
    bias_two = jnp.zeros(ln1_gain.shape, jnp.float32)
    grad_cls_in = jnp.zeros(cls_in.shape, jnp.float32)
    grad_pool = jnp.zeros(pool_query.shape, jnp.float32)
    grad_mid = jnp.zeros(cls_mid.shape, jnp.float32)
    grad_top = jnp.zeros(cls_out.shape, jnp.float32)
    out_list = []
    loss_list = []
    grad_list = []
    for micro_index in range(tokens.shape[0]):
        inputs_here = tokens[micro_index, 0]
        inputs_full = features(inputs_here)
        qkv_rows = jnp.dot(inputs_full, qkv_full, preferred_element_type=jnp.float32).astype(
            jnp.bfloat16
        )
        query_heads = qkv_rows[:, :head_cols].reshape(row_count, heads_here, HDIM)
        pair_here = qkv_rows[:, head_cols:]
        start_state = (
            jnp.full((heads_here, row_count), -1e30, jnp.float32),
            jnp.zeros((heads_here, row_count), jnp.float32),
            jnp.zeros((row_count, heads_here, HDIM), jnp.float32),
        )
        pair_all = lax.all_gather(pair_here, "dp", axis=0, tiled=True)
        row_top, row_total, weighted = fold_keys(start_state, pair_all, query_heads)
        log_total = row_top + jnp.log(row_total)
        attended = weighted / jnp.transpose(row_total)[:, :, None]
        attended_low = attended.reshape(row_count, head_cols).astype(jnp.bfloat16)
        branch = spread_sum(jnp.dot(attended_low, out_full, preferred_element_type=jnp.float32))
        normed, centred_one, inv_one = norm_forward(
            inputs_here.astype(jnp.float32) + branch, ln1_gain, ln1_bias
        )
        normed_full = features(normed.astype(jnp.bfloat16))
        up_pre = jnp.dot(normed_full, up_full, preferred_element_type=jnp.float32)
        activated, gelu_back = jax.vjp(exact_gelu, up_pre)
        activated_low = activated.astype(jnp.bfloat16)
        down_out = spread_sum(jnp.dot(activated_low, down_full, preferred_element_type=jnp.float32))
        outputs, centred_two, inv_two = norm_forward(normed + down_out, ln2_gain, ln2_bias)
        outputs_low = outputs.astype(jnp.bfloat16)
        out_list.append(outputs_low)
        cls_proj = lax.psum(
            jnp.dot(outputs_low, cls_in, preferred_element_type=jnp.float32).astype(jnp.bfloat16),
            "cols",
        ).astype(jnp.float32)
        pool_heads = cls_proj.reshape(row_count, POOL_HEADS, pool_dim)
        pool_scores = (
            jnp.einsum("lpd,pd->lp", pool_heads, pool_query, precision=highest) / pool_root
        )
        local_top = jnp.max(pool_scores, axis=0)
        pool_exp = jnp.exp(pool_scores - local_top)
        pool_top, pool_total, pool_sum = merged(
            (
                local_top,
                jnp.sum(pool_exp, axis=0),
                jnp.einsum("lp,lpd->pd", pool_exp, pool_heads, precision=highest),
            ),
            "dp",
            pool_combine,
        )
        pooled = pool_sum / pool_total[:, None]
        pool_weights = jnp.exp(pool_scores - pool_top) / pool_total
        pooled_row = pooled.reshape(1, CLS_D)
        hidden_cls = jnp.tanh(jnp.dot(pooled_row, cls_mid, precision=highest))
        logits = jnp.dot(hidden_cls, cls_out, precision=highest)[0]
        target_hit = lax.iota(jnp.int32, CLASSES) == labels[micro_index, 0]
        loss_list.append(jax.nn.logsumexp(logits) - jnp.sum(jnp.where(target_hit, logits, 0.0)))
        dlogits = jax.nn.softmax(logits) - target_hit.astype(jnp.float32)
        grad_top = grad_top + hidden_cls[0][:, None] * dlogits[None, :]
        dhidden = jnp.dot(cls_out, dlogits, precision=highest)
        dpre_tanh = dhidden * (1.0 - hidden_cls[0] * hidden_cls[0])
        grad_mid = grad_mid + pooled_row[0][:, None] * dpre_tanh[None, :]
        dpooled = jnp.dot(cls_mid, dpre_tanh, precision=highest).reshape(POOL_HEADS, pool_dim)
        dweights = jnp.einsum("lpd,pd->lp", pool_heads, dpooled, precision=highest)
        centre_term = jnp.sum(pooled * dpooled, axis=1)
        dpool_scores = pool_weights * (dweights - centre_term)
        dheads = (
            pool_weights[:, :, None] * dpooled[None]
            + dpool_scores[:, :, None] * (pool_query / pool_root)[None]
        )
        grad_pool = (
            grad_pool
            + jnp.einsum("lp,lpd->pd", dpool_scores, pool_heads, precision=highest) / pool_root
        )
        dproj_low = dheads.reshape(row_count, CLS_D).astype(jnp.bfloat16)
        grad_cls_in = grad_cls_in + dot_rows(outputs_low, dproj_low)
        upstream = cotangent[micro_index, 0].astype(jnp.float32) + dot_cols(dproj_low, cls_in)
        gain_two = gain_two + jnp.sum(upstream * centred_two, axis=0)
        bias_two = bias_two + jnp.sum(upstream, axis=0)
        dhidden_two = norm_backward(upstream, centred_two, inv_two, ln2_gain)
        ddown_full = features(dhidden_two.astype(jnp.bfloat16))
        grad_down_now = dot_rows(activated_low, ddown_full)
        dact_grad = dot_cols(ddown_full, down_full)
        dup_low = gelu_back(dact_grad)[0].astype(jnp.bfloat16)
        grad_up_now = dot_rows(normed_full, dup_low)
        dnormed = dhidden_two + spread_sum(dot_cols(dup_low, up_full))
        gain_one = gain_one + jnp.sum(dnormed * centred_one, axis=0)
        bias_one = bias_one + jnp.sum(dnormed, axis=0)
        dhidden_one = norm_backward(dnormed, centred_one, inv_one, ln1_gain)
        dattn_full = features(dhidden_one.astype(jnp.bfloat16))
        grad_attn_now = dot_rows(attended_low, dattn_full)
        dattended = dot_cols(dattn_full, out_full).astype(jnp.bfloat16)
        grad_heads = dattended.reshape(row_count, heads_here, HDIM)
        delta_rows = jnp.transpose(jnp.sum(grad_heads.astype(jnp.float32) * attended, axis=2))
        dquery, pair_terms = joint_grads(pair_all, query_heads, grad_heads, log_total, delta_rows)
        dpair_sum = lax.psum_scatter(
            pair_terms.astype(jnp.bfloat16), "dp", scatter_dimension=0, tiled=True
        ).astype(jnp.float32)
        dqkv_low = jnp.concatenate(
            [dquery.reshape(row_count, head_cols), dpair_sum], axis=1
        ).astype(jnp.bfloat16)
        grad_qkv_now = dot_rows(inputs_full, dqkv_low)
        grad_list.append(dhidden_one + spread_sum(dot_cols(dqkv_low, qkv_full)))
        micro_grads = (grad_qkv_now, grad_attn_now, grad_up_now, grad_down_now)
        local_grads = tuple(
            (left_val + right_val for left_val, right_val in zip(local_grads, micro_grads))
        )
    final_set = reduce_weights(local_grads, head_cols)
    lead_mask = (lax.axis_index("dp") == 0).astype(jnp.float32)
    sum_gain1, sum_bias1, sum_gain2, sum_bias2, sum_cls_in, sum_pool, sum_mid, sum_top = lax.psum(
        (
            gain_one,
            bias_one,
            gain_two,
            bias_two,
            grad_cls_in,
            grad_pool,
            grad_mid * lead_mask,
            grad_top * lead_mask,
        ),
        ("dp", "rows"),
    )
    return (
        jnp.stack(out_list)[:, None],
        jnp.stack(loss_list)[:, None],
        jnp.stack(grad_list)[:, None],
        final_set[0],
        final_set[1],
        final_set[2],
        final_set[3],
        final_set[4],
        final_set[5],
        sum_gain1,
        sum_bias1,
        sum_gain2,
        sum_bias2,
        sum_cls_in,
        sum_pool,
        sum_mid,
        sum_top,
    )


def solution(mesh):
    placed = (
        P(None, "rows", "dp", "cols"),
        P(None, "rows", "dp", "cols"),
        P(None, "rows"),
        P("rows", "cols"),
        P("rows", "cols"),
        P("rows", "cols"),
        P("cols", "rows"),
        P("rows", "cols"),
        P("cols", "rows"),
        P("cols"),
        P("cols"),
        P("cols"),
        P("cols"),
        P("cols", None),
        P(),
        P(),
        P(),
    )
    return jax.shard_map(
        body,
        mesh=mesh,
        in_specs=placed,
        out_specs=(
            P(None, "rows", "dp", "cols"),
            P(None, "rows"),
            P(None, "rows", "dp", "cols"),
            P("rows", "cols"),
            P("rows", "cols"),
            P("rows", "cols"),
            P("cols", "rows"),
            P("rows", "cols"),
            P("cols", "rows"),
            P("cols"),
            P("cols"),
            P("cols"),
            P("cols"),
            P("cols", None),
            P(),
            P(),
            P(),
        ),
        check_vma=False,
    )
```

profile of v0, /device:TPU:0, one launch (start us, length us, event | category | flops | bytes accessed | tf_op | source)
XLA Modules:
  0.0 1253.1 jit_solution(9522413399864442502)
XLA Ops:
  16.7 16.3 %all-gather.2 = bf16[1,1,256,768]{2,3,1,0:T(8,128)(2,1)S(1)} all-gather(bf16[1,1,256,192]{2,3,1,0:T(8,128)(2,1)S(1)} %get-tuple-element.1210), channel_id=4, replica_groups=mesh['dp'=4,'rows'=2,'cols'=4] {'cols'}, dimensions={3}, use_global_device_ids=true | all-gather | bytes 491520 | tf_op jit(solution)/shard_map/all_gather | solution.py:31
  34.1 15.1 %all_gather.163 = bf16[1024,384]{0,1:T(8,128)(2,1)S(1)} all-gather(bf16[256,384]{0,1:T(8,128)(2,1)S(1)} %slice.188), channel_id=1, replica_groups=mesh['dp'=4,'rows'=2,'cols'=4] {'dp'}, dimensions={0}, use_global_device_ids=true | all-gather | bytes 983040 | tf_op jit(solution)/shard_map/all_gather | solution.py:281
  58.4 18.4 %all-gather.3 = bf16[1,1,256,768]{2,3,1,0:T(8,128)(2,1)S(1)} all-gather(bf16[1,1,256,192]{2,3,1,0:T(8,128)(2,1)} %get-tuple-element.1207), channel_id=5, replica_groups=mesh['dp'=4,'rows'=2,'cols'=4] {'cols'}, dimensions={3}, use_global_device_ids=true | all-gather | bytes 491520 | tf_op jit(solution)/shard_map/all_gather | solution.py:31
  78.6 14.7 %all_gather.166 = bf16[1024,384]{0,1:T(8,128)(2,1)S(1)} all-gather(bf16[256,384]{0,1:T(8,128)(2,1)S(1)} %slice.192), channel_id=1, replica_groups=mesh['dp'=4,'rows'=2,'cols'=4] {'dp'}, dimensions={0}, use_global_device_ids=true | all-gather | bytes 983040 | tf_op jit(solution)/shard_map/all_gather | solution.py:281
  110.9 15.6 %all_gather.164 = bf16[256,768]{0,1:T(8,128)(2,1)} all-gather(bf16[256,192]{0,1:T(8,128)(2,1)S(1)} %fusion.175), channel_id=1, replica_groups=mesh['dp'=4,'rows'=2,'cols'=4] {'cols'}, dimensions={1}, use_global_device_ids=true | all-gather | bytes 491520 | tf_op jit(solution)/shard_map/all_gather | solution.py:31
  169.3 15.1 %all-gather.1 = bf16[1,1,256,768]{2,3,1,0:T(8,128)(2,1)S(1)} all-gather(bf16[1,1,256,192]{2,3,1,0:T(8,128)(2,1)} %get-tuple-element.1208), channel_id=3, replica_groups=mesh['dp'=4,'rows'=2,'cols'=4] {'cols'}, dimensions={3}, use_global_device_ids=true | all-gather | bytes 491520 | tf_op jit(solution)/shard_map/all_gather | solution.py:31
  186.1 14.7 %all_gather.160 = bf16[1024,384]{0,1:T(8,128)(2,1)S(1)} all-gather(bf16[256,384]{0,1:T(8,128)(2,1)S(1)} %slice.184), channel_id=1, replica_groups=mesh['dp'=4,'rows'=2,'cols'=4] {'dp'}, dimensions={0}, use_global_device_ids=true | all-gather | bytes 983040 | tf_op jit(solution)/shard_map/all_gather | solution.py:281
  207.1 16.4 %all-gather = bf16[1,1,256,768]{2,3,1,0:T(8,128)(2,1)S(1)} all-gather(bf16[1,1,256,192]{2,3,1,0:T(8,128)(2,1)} %get-tuple-element.1209), channel_id=2, replica_groups=mesh['dp'=4,'rows'=2,'cols'=4] {'cols'}, dimensions={3}, use_global_device_ids=true | all-gather | bytes 491520 | tf_op jit(solution)/shard_map/all_gather | solution.py:31
  225.3 14.3 %all_gather.154 = bf16[1024,384]{0,1:T(8,128)(2,1)S(1)} all-gather(bf16[256,384]{0,1:T(8,128)(2,1)S(1)} %slice.180), channel_id=1, replica_groups=mesh['dp'=4,'rows'=2,'cols'=4] {'dp'}, dimensions={0}, use_global_device_ids=true | all-gather | bytes 983040 | tf_op jit(solution)/shard_map/all_gather | solution.py:281
  324.1 14.3 %all_gather.196 = bf16[256,768]{0,1:T(8,128)(2,1)S(1)} all-gather(bf16[256,192]{0,1:T(8,128)(2,1)S(1)} %fusion.259), channel_id=1, replica_groups=mesh['dp'=4,'rows'=2,'cols'=4] {'cols'}, dimensions={1}, use_global_device_ids=true | all-gather | bytes 491520 | tf_op jit(solution)/shard_map/all_gather | solution.py:31
  343.8 18.3 %reduce-scatter.65.cloned.1.call-done = bf16[256,192]{0,1:T(8,128)(2,1)} async-done(((bf16[256,768]{0,1:T(8,128)(2,1)}), bf16[256,192]{0,1:T(8,128)(2,1)}) %reduce-scatter.65.cloned.1.call-update) | async-done | bytes 98320 | tf_op jit(solution)/shard_map/reduce_scatter | solution.py:35
  376.2 14.3 %all_gather.156 = bf16[256,768]{0,1:T(8,128)(2,1)S(1)} all-gather(bf16[256,192]{0,1:T(8,128)(2,1)S(1)} %fusion.173), channel_id=1, replica_groups=mesh['dp'=4,'rows'=2,'cols'=4] {'cols'}, dimensions={1}, use_global_device_ids=true | all-gather | bytes 491520 | tf_op jit(solution)/shard_map/all_gather | solution.py:31
  400.2 17.9 %reduce-scatter.39.cloned.1.call-done = bf16[256,192]{0,1:T(8,128)(2,1)} async-done(((bf16[256,768]{0,1:T(8,128)(2,1)}), bf16[256,192]{0,1:T(8,128)(2,1)}) %reduce-scatter.39.cloned.1.call-update) | async-done | bytes 98320 | tf_op jit(solution)/shard_map/reduce_scatter | solution.py:35
  420.8 14.3 %all_gather.167 = bf16[256,768]{0,1:T(8,128)(2,1)S(1)} all-gather(bf16[256,192]{0,1:T(8,128)(2,1)S(1)} %get-tuple-element.1195), channel_id=1, replica_groups=mesh['dp'=4,'rows'=2,'cols'=4] {'cols'}, dimensions={1}, use_global_device_ids=true | all-gather | bytes 491520 | tf_op jit(solution)/shard_map/all_gather | solution.py:31
  441.9 15.2 %all_gather.161 = bf16[256,768]{0,1:T(8,128)(2,1)S(1)} all-gather(bf16[256,192]{0,1:T(8,128)(2,1)} %get-tuple-element.1194), channel_id=1, replica_groups=mesh['dp'=4,'rows'=2,'cols'=4] {'cols'}, dimensions={1}, use_global_device_ids=true | all-gather | bytes 491520 | tf_op jit(solution)/shard_map/all_gather | solution.py:31
  463.8 21.3 %reduce-scatter.43.cloned.1.call-done = bf16[256,192]{0,1:T(8,128)(2,1)} async-done(((bf16[256,768]{0,1:T(8,128)(2,1)}), bf16[256,192]{0,1:T(8,128)(2,1)}) %reduce-scatter.43.cloned.1.call-update) | async-done | bytes 98320 | tf_op jit(solution)/shard_map/reduce_scatter | solution.py:35
  504.0 34.7 %all-reduce.30.cloned.1.call-done = (bf16[256,2,64]{0,2,1:T(8,128)(2,1)}, bf16[256,2,64]{0,2,1:T(8,128)(2,1)}, bf16[256,2,64]{0,2,1:T(8,128)(2,1)}) async-done(((bf16[256,2,64]{0,2,1:T(8,128)(2,1)}, bf16[256,2,64]{0,2,1:T(8,128)(2,1)}, bf16[256,2,64]{0,2,1:T(8,128)(2,1)}), (bf16[256,2,64]{0,2,1:T(8,128)(2,1)}, bf16[256,2,64]{0,2,1:T(8,128)(2,1)}, ...) | async-done | bytes 196624 | tf_op jit(solution)/shard_map/psum | solution.py:298
  705.4 16.0 %all_gather.194 = bf16[256,768]{0,1:T(8,128)(2,1)} all-gather(bf16[256,192]{0,1:T(8,128)(2,1)S(1)} %get-tuple-element.1233), channel_id=1, replica_groups=mesh['dp'=4,'rows'=2,'cols'=4] {'cols'}, dimensions={1}, use_global_device_ids=true | all-gather | bytes 491520 | tf_op jit(solution)/shard_map/all_gather | solution.py:31
  721.3 14.5 %all_gather.198 = bf16[256,768]{0,1:T(8,128)(2,1)S(1)} all-gather(bf16[256,192]{0,1:T(8,128)(2,1)S(1)} %get-tuple-element.1234), channel_id=1, replica_groups=mesh['dp'=4,'rows'=2,'cols'=4] {'cols'}, dimensions={1}, use_global_device_ids=true | all-gather | bytes 491520 | tf_op jit(solution)/shard_map/all_gather | solution.py:31
  745.8 13.5 %reduce-scatter.71.cloned.1.call-done = bf16[256,192]{0,1:T(8,128)(2,1)} async-done(((bf16[256,768]{0,1:T(8,128)(2,1)}), bf16[256,192]{0,1:T(8,128)(2,1)}) %reduce-scatter.71.cloned.1.call-update) | async-done | bytes 98320 | tf_op jit(solution)/shard_map/reduce_scatter | solution.py:35
  762.1 15.4 %all_gather.192 = bf16[256,768]{0,1:T(8,128)(2,1)S(1)} all-gather(bf16[256,192]{0,1:T(8,128)(2,1)S(1)} %get-tuple-element.1232), channel_id=1, replica_groups=mesh['dp'=4,'rows'=2,'cols'=4] {'cols'}, dimensions={1}, use_global_device_ids=true | all-gather | bytes 491520 | tf_op jit(solution)/shard_map/all_gather | solution.py:31
  782.8 21.8 %reduce-scatter.53.cloned.1.call-done = bf16[256,192]{0,1:T(8,128)(2,1)} async-done(((bf16[256,768]{0,1:T(8,128)(2,1)}), bf16[256,192]{0,1:T(8,128)(2,1)}) %reduce-scatter.53.cloned.1.call-update) | async-done | bytes 98320 | tf_op jit(solution)/shard_map/reduce_scatter | solution.py:35
  828.2 14.3 %all_gather.195 = bf16[256,768]{0,1:T(8,128)(2,1)S(1)} all-gather(bf16[256,192]{0,1:T(8,128)(2,1)S(1)} %get-tuple-element.1203), channel_id=1, replica_groups=mesh['dp'=4,'rows'=2,'cols'=4] {'cols'}, dimensions={1}, use_global_device_ids=true | all-gather | bytes 491520 | tf_op jit(solution)/shard_map/all_gather | solution.py:31
  851.5 14.2 %all_gather.193 = bf16[256,768]{0,1:T(8,128)(2,1)S(1)} all-gather(bf16[256,192]{0,1:T(8,128)(2,1)S(1)} %get-tuple-element.1201), channel_id=1, replica_groups=mesh['dp'=4,'rows'=2,'cols'=4] {'cols'}, dimensions={1}, use_global_device_ids=true | all-gather | bytes 491520 | tf_op jit(solution)/shard_map/all_gather | solution.py:31
  871.7 15.3 %all_gather.197 = bf16[256,768]{0,1:T(8,128)(2,1)S(1)} all-gather(bf16[256,192]{0,1:T(8,128)(2,1)} %get-tuple-element.1204), channel_id=1, replica_groups=mesh['dp'=4,'rows'=2,'cols'=4] {'cols'}, dimensions={1}, use_global_device_ids=true | all-gather | bytes 491520 | tf_op jit(solution)/shard_map/all_gather | solution.py:31
  892.5 14.8 %all_gather.199 = bf16[256,768]{0,1:T(8,128)(2,1)S(1)} all-gather(bf16[256,192]{0,1:T(8,128)(2,1)} %get-tuple-element.1202), channel_id=1, replica_groups=mesh['dp'=4,'rows'=2,'cols'=4] {'cols'}, dimensions={1}, use_global_device_ids=true | all-gather | bytes 491520 | tf_op jit(solution)/shard_map/all_gather | solution.py:31
  938.7 24.4 %reduce-scatter.73.cloned.1.call-done = bf16[256,384]{0,1:T(8,128)(2,1)} async-done(((bf16[1024,384]{0,1:T(8,128)(2,1)}), bf16[256,384]{0,1:T(8,128)(2,1)}) %reduce-scatter.73.cloned.1.call-update) | async-done | bytes 196624 | tf_op jit(solution)/shard_map/reduce_scatter | solution.py:362
  1037.2 26.1 %all-reduce.8 = (f32[192]{0:T(256)}, f32[192]{0:T(256)}, f32[192]{0:T(256)}, f32[192]{0:T(256)}, f32[2,64]{1,0:T(2,128)}, /*index=5*/f32[128,14]{0,1:T(8,128)}) all-reduce(f32[192]{0:T(256)S(1)} %add_add_fusion.3, f32[192]{0:T(256)S(1)} %add_add_fusion.2, ...), channel_id=1, replica_groups=mesh['dp'=4,'rows'=2,'cols'=4] {'dp','rows'}, use_global_device_ids=true, to_apply=%region_152.153 | all-reduce | flops 2688 | bytes 21504 | tf_op jit(solution)/shard_map/psum | solution.py:376
  1077.8 20.3 %reduce-scatter.75.cloned.1.call-done = bf16[256,192]{0,1:T(8,128)(2,1)} async-done(((bf16[256,768]{0,1:T(8,128)(2,1)}), bf16[256,192]{0,1:T(8,128)(2,1)}) %reduce-scatter.75.cloned.1.call-update) | async-done | bytes 98320 | tf_op jit(solution)/shard_map/reduce_scatter | solution.py:35
  1098.0 21.9 %reduce-scatter.69.cloned.1.call-done = bf16[256,192]{0,1:T(8,128)(2,1)} async-done(((bf16[256,768]{0,1:T(8,128)(2,1)}), bf16[256,192]{0,1:T(8,128)(2,1)}) %reduce-scatter.69.cloned.1.call-update) | async-done | bytes 98320 | tf_op jit(solution)/shard_map/reduce_scatter | solution.py:35
  1122.1 64.6 %all-reduce.32.cloned.1.call-done = (bf16[384,192]{0,1:T(8,128)(2,1)}, bf16[384,192]{0,1:T(8,128)(2,1)}, bf16[384,192]{0,1:T(8,128)(2,1)}, bf16[192,384]{1,0:T(8...) async-done(((bf16[384,192]{0,1:T(8,128)(2,1)}, bf16[384,192]{0,1:T(8,128)(2,1)}, bf16[384,192]{0,1:T(8,128)(2,1)}, bf16[192,384]{1,0:T(8,128)(2,1)}, ...) | async-done | bytes 1769488 | tf_op jit(solution)/shard_map/psum | solution.py:209
  1194.0 48.5 %all-reduce.28.cloned.1.call-done = (f32[192,128]{1,0:T(8,128)}, f32[128,128]{1,0:T(8,128)}) async-done(((f32[192,128]{1,0:T(8,128)}, f32[128,128]{1,0:T(8,128)}), (f32[192,128]{1,0:T(8,128)}, f32[128,128]{1,0:T(8,128)})) %all-reduce.28.cloned.1.call-update) | async-done | bytes 163856 | tf_op jit(solution)/shard_map/psum | solution.py:376
  (927 shorter events, 617.7 us)
Async XLA Ops:
  8.0 89.8 %reduce-scatter.45.cloned.1.call-start = ((), (), s32[]{:S(2)}) async-start(), calls=%async_computation.32 | async-start | bytes 491520 | tf_op jit(solution)/shard_map/reduce_scatter | solution.py:35
  57.2 69.3 %all-gather.23.cloned.1.call-start = ((), (), s32[]{:S(2)}) async-start(), calls=%async_computation.27 | async-start | bytes 1769472 | tf_op jit(solution)/shard_map/all_gather | solution.py:242
  57.8 73.3 %all-gather.25.cloned.1.call-start = ((), (), s32[]{:S(2)}) async-start(), calls=%async_computation.28 | async-start | bytes 1769472 | tf_op jit(solution)/shard_map/all_gather | solution.py:243
  58.3 94.0 %reduce-scatter.47.cloned.1.call-start = ((), (), s32[]{:S(2)}) async-start(), calls=%async_computation.33 | async-start | bytes 491520 | tf_op jit(solution)/shard_map/reduce_scatter | solution.py:35
  133.9 117.9 %all-reduce.26.cloned.1.call-start = ((), (), s32[]{:S(2)}) async-start(), calls=%async_computation.36 | async-start | bytes 131072 | tf_op jit(solution)/shard_map/psum | solution.py:298
  167.2 176.5 %reduce-scatter.49.cloned.1.call-start = ((), (), s32[]{:S(2)}) async-start(), calls=%async_computation.34 | async-start | bytes 491520 | tf_op jit(solution)/shard_map/reduce_scatter | solution.py:35
  169.2 174.5 %reduce-scatter.41.cloned.1.call-start = ((), (), s32[]{:S(2)}) async-start(), calls=%async_computation.30 | async-start | bytes 491520 | tf_op jit(solution)/shard_map/reduce_scatter | solution.py:35
  207.1 136.7 %reduce-scatter.37.cloned.1.call-start = ((), (), s32[]{:S(2)}) async-start(), calls=%async_computation.26 | async-start | bytes 491520 | tf_op jit(solution)/shard_map/reduce_scatter | solution.py:35
  245.8 116.2 %reduce-scatter.65.cloned.1.call-start = ((), (), s32[]{:S(2)}) async-start(), calls=%async_computation.43 | async-start | bytes 491520 | tf_op jit(solution)/shard_map/reduce_scatter | solution.py:35
  343.6 74.5 %reduce-scatter.39.cloned.1.call-start = ((), (), s32[]{:S(2)}) async-start(), calls=%async_computation.29 | async-start | bytes 491520 | tf_op jit(solution)/shard_map/reduce_scatter | solution.py:35
  397.2 66.6 %reduce-scatter.51.cloned.1.call-start = ((), (), s32[]{:S(2)}) async-start(), calls=%async_computation.35 | async-start | bytes 491520 | tf_op jit(solution)/shard_map/reduce_scatter | solution.py:35
  441.9 43.3 %reduce-scatter.43.cloned.1.call-start = ((), (), s32[]{:S(2)}) async-start(), calls=%async_computation.31 | async-start | bytes 491520 | tf_op jit(solution)/shard_map/reduce_scatter | solution.py:35
  463.8 75.0 %all-reduce.30.cloned.1.call-start = ((), (), s32[]{:S(2)}) async-start(), calls=%async_computation.56 | async-start | bytes 393216 | tf_op jit(solution)/shard_map/psum | solution.py:298
  504.0 255.4 %reduce-scatter.71.cloned.1.call-start = ((), (), s32[]{:S(2)}) async-start(), calls=%async_computation.46 | async-start | bytes 491520 | tf_op jit(solution)/shard_map/reduce_scatter | solution.py:35
  741.0 41.8 %reduce-scatter.59.cloned.1.call-start = ((), (), s32[]{:S(2)}) async-start(), calls=%async_computation.40 | async-start | bytes 491520 | tf_op jit(solution)/shard_map/reduce_scatter | solution.py:35
  745.8 58.9 %reduce-scatter.53.cloned.1.call-start = ((), (), s32[]{:S(2)}) async-start(), calls=%async_computation.37 | async-start | bytes 491520 | tf_op jit(solution)/shard_map/reduce_scatter | solution.py:35
  782.8 149.2 %reduce-scatter.61.cloned.1.call-start = ((), (), s32[]{:S(2)}) async-start(), calls=%async_computation.41 | async-start | bytes 983040 | tf_op jit(solution)/shard_map/reduce_scatter | solution.py:362
  849.4 84.0 %reduce-scatter.55.cloned.1.call-start = ((), (), s32[]{:S(2)}) async-start(), calls=%async_computation.38 | async-start | bytes 983040 | tf_op jit(solution)/shard_map/reduce_scatter | solution.py:362
  871.7 64.5 %reduce-scatter.67.cloned.1.call-start = ((), (), s32[]{:S(2)}) async-start(), calls=%async_computation.44 | async-start | bytes 983040 | tf_op jit(solution)/shard_map/reduce_scatter | solution.py:362
  892.4 70.7 %reduce-scatter.73.cloned.1.call-start = ((), (), s32[]{:S(2)}) async-start(), calls=%async_computation.47 | async-start | bytes 983040 | tf_op jit(solution)/shard_map/reduce_scatter | solution.py:362
  912.7 78.5 %reduce-scatter.85.cloned.1.call-start = ((), (), s32[]{:S(2)}) async-start(), calls=%async_computation.53 | async-start | bytes 589824
  919.8 73.2 %reduce-scatter.87.cloned.1.call-start = ((), (), s32[]{:S(2)}) async-start(), calls=%async_computation.54 | async-start | bytes 1769472
  926.0 70.4 %reduce-scatter.79.cloned.1.call-start = ((), (), s32[]{:S(2)}) async-start(), calls=%async_computation.50 | async-start | bytes 589824
  966.7 40.9 %reduce-scatter.81.cloned.1.call-start = ((), (), s32[]{:S(2)}) async-start(), calls=%async_computation.51 | async-start | bytes 589824
  967.7 51.0 %reduce-scatter.83.cloned.1.call-start = ((), (), s32[]{:S(2)}) async-start(), calls=%async_computation.52 | async-start | bytes 589824
  973.1 57.9 %reduce-scatter.77.cloned.1.call-start = ((), (), s32[]{:S(2)}) async-start(), calls=%async_computation.49 | async-start | bytes 1769472 | tf_op jit(solution)/shard_map/reduce_scatter | solution.py:201
  976.7 86.5 %reduce-scatter.63.cloned.1.call-start = ((), (), s32[]{:S(2)}) async-start(), calls=%async_computation.42 | async-start | bytes 491520 | tf_op jit(solution)/shard_map/reduce_scatter | solution.py:35
  979.4 97.2 %reduce-scatter.57.cloned.1.call-start = ((), (), s32[]{:S(2)}) async-start(), calls=%async_computation.39 | async-start | bytes 491520 | tf_op jit(solution)/shard_map/reduce_scatter | solution.py:35
  981.0 117.1 %reduce-scatter.75.cloned.1.call-start = ((), (), s32[]{:S(2)}) async-start(), calls=%async_computation.48 | async-start | bytes 491520 | tf_op jit(solution)/shard_map/reduce_scatter | solution.py:35
  982.7 137.3 %reduce-scatter.69.cloned.1.call-start = ((), (), s32[]{:S(2)}) async-start(), calls=%async_computation.45 | async-start | bytes 491520 | tf_op jit(solution)/shard_map/reduce_scatter | solution.py:35
  984.1 202.6 %all-reduce.32.cloned.1.call-start = ((), (), s32[]{:S(2)}) async-start(), calls=%async_computation.57 | async-start | bytes 3538944 | tf_op jit(solution)/shard_map/psum | solution.py:209
  1031.1 211.4 %all-reduce.28.cloned.1.call-start = ((), (), s32[]{:S(2)}) async-start(), calls=%async_computation.55 | async-start | bytes 327680 | tf_op jit(solution)/shard_map/psum | solution.py:376
  (246 other events, 4210.8 us)
Sparse Core Ops, SparseCore 0:
  57.3 22.7 reduce-scatter.44
  134.0 18.3 reduce-scatter.46
  167.3 33.7 all-reduce.25
  203.3 21.5 reduce-scatter.48
  227.6 18.7 reduce-scatter.40
  249.1 19.2 reduce-scatter.36
  343.7 18.2 reduce-scatter.64
  397.3 20.7 reduce-scatter.38
  442.0 20.6 reduce-scatter.50
  465.4 19.7 reduce-scatter.42
  504.1 34.5 all-reduce.29
  741.1 18.1 reduce-scatter.70
  762.2 20.4 reduce-scatter.58
  785.4 19.2 reduce-scatter.52
Sparse Core Ops, SparseCore 1:
  59.2 9.0 all-gather.22
  69.7 10.2 all-gather.24
  849.5 26.0 reduce-scatter.60
  878.4 26.0 reduce-scatter.54
  908.0 26.0 reduce-scatter.66
  937.0 26.0 reduce-scatter.72
  965.2 7.7 reduce-scatter.84
  975.7 9.5 reduce-scatter.86
  987.4 9.0 reduce-scatter.78
  998.7 8.8 reduce-scatter.80
  1009.7 8.8 reduce-scatter.82
  1021.5 9.5 reduce-scatter.76
  1033.2 22.0 reduce-scatter.62
  1057.6 19.0 reduce-scatter.56
  1078.9 19.1 reduce-scatter.74
  1100.9 19.0 reduce-scatter.68
  1124.4 62.2 all-reduce.31
  1190.5 52.0 all-reduce.27
where the time goes:
time: 1270 us; the launch traced here: 1250 us
  blocking collectives  458 us (36%)
  waiting for transfers between devices  364 us (29%)
  matrix products  158 us (12%)
  other arithmetic  144 us (11%)
  local copies, waits for them, and re-layouts  96.8 us (8%)
  between operations  29.9 us (2%)
    all_gather x16, blocking collectives, features(): return lax.all_gather(shard_part, 'cols', axis=1, tiled=True)  244 us
    reduce_scatter x16, waiting for transfers between devices, spread_sum(): lax.psum_scatter(partial_value.astype(jnp.bfloat16), 'cols', scatter_dime...  160 us
    psum x7, blocking collectives, token_sums(): return lax.psum((plain_sum, cross_sum), 'cols')  69.3 us
    psum x1, waiting for transfers between devices, reduce_weights(): lax.psum(part_q.astype(jnp.bfloat16), 'dp').astype(jnp.float32)  64.6 us
    unnamed x523, local copies, waits for them, and re-layouts  63 us
    all_gather x4, blocking collectives, body(): pair_all = lax.all_gather(pair_here, 'dp', axis=0, tiled=True)  58.7 us
    psum x1, waiting for transfers between devices, body(): lax.psum((gain_one, bias_one, gain_two, bias_two, grad_cls_in, grad_pool,...  48.5 us
    psum x2, waiting for transfers between devices, body(): lax.psum(jnp.dot(outputs_low, cls_in, preferred_element_type=jnp.float32)...  34.7 us
  transfers between devices with their start and end apart: 32, of which 17 were waited for; matrix products, arithmetic and copies ran while one was open for 15% of the time, Pallas kernels for 0%

commit v1 on v0

--- a/solution.py
+++ b/solution.py
@@ -3,7 +3,287 @@
 import jax
 import jax.numpy as jnp
 from jax import lax
+from jax.experimental import pallas as pl
+from jax.experimental.pallas import tpu as pltpu
 from jax.sharding import PartitionSpec as P
+
+MESH = pl.DeviceIdType.MESH
+VMEM_GRANT = 60 * 1024 * 1024
+HALF = 384
+
+
+def split_rows(count):
+    first = (count // 32) * 16 if (count // 2) % 16 else count // 2
+    return (first, count - first)
+
+
+def position():
+    return (lax.axis_index("dp"), lax.axis_index("rows"), lax.axis_index("cols"))
+
+
+def plane_x(p):
+    return p + 1 - 2 * (p % 2)
+
+
+def plane_y(p):
+    return (p + 2) % 4
+
+
+def greet(devices):
+    barrier = pltpu.get_barrier_semaphore()
+    for device in devices:
+        pl.semaphore_signal(barrier, inc=1, device_id=device, device_id_type=MESH)
+    pl.semaphore_wait(barrier, len(devices))
+
+
+def remote(src, dst, send_sem, recv_sem, device):
+    return pltpu.make_async_remote_copy(
+        src_ref=src,
+        dst_ref=dst,
+        send_sem=send_sem,
+        recv_sem=recv_sem,
+        device_id=device,
+        device_id_type=MESH,
+    )
+
+
+def comm_call(kernel, args, outs, scratch, ident):
+    any_spec = pl.BlockSpec(memory_space=pl.ANY)
+    return pl.pallas_call(
+        kernel,
+        out_shape=outs,
+        in_specs=[any_spec] * len(args),
+        out_specs=[any_spec] * len(outs),
+        scratch_shapes=scratch,
+        compiler_params=pltpu.CompilerParams(
+            collective_id=ident, has_side_effects=True, vmem_limit_bytes=VMEM_GRANT
+        ),
+    )(*args)
+
+
+def gather_kernel(swaps, casts, weights):
+    def kernel(*refs):
+        total = len(swaps) + len(casts) + len(weights)
+        ins = refs[:total]
+        outs = refs[total : 2 * total]
+        zsend, zrecv, wsend, wrecv, local_sem = refs[2 * total :]
+        p, r, c = position()
+        px, py = plane_x(p), plane_y(p)
+        others = [(p, r, (c + k) % 4) for k in range(1, 4)]
+        twin = (p, 1 - r, c)
+        greet(others + [(px, r, c), (py, r, c), twin])
+        small = len(swaps) + len(casts)
+        sent = []
+        locals_ = []
+
+        def keep(src, dst, index):
+            copy = pltpu.make_async_copy(src, dst, local_sem.at[index])
+            copy.start()
+            locals_.append(copy)
+
+        for index in range(small):
+            for k in range(1, 4):
+                peer = (c + k) % 4
+                src = ins[index].at[peer] if index < len(swaps) else ins[index]
+                copy = remote(
+                    src,
+                    outs[index].at[c],
+                    zsend.at[index, k - 1],
+                    zrecv.at[index, 3 - k],
+                    (p, r, peer),
+                )
+                copy.start()
+                sent.append(copy)
+            keep(
+                ins[index].at[c] if index < len(swaps) else ins[index], outs[index].at[c], index
+            )
+
+        lanes = pl.ds(pl.multiple_of(r * HALF, HALF), HALF)
+        other_lanes = pl.ds(pl.multiple_of((1 - r) * HALF, HALF), HALF)
+
+        def plan(g):
+            src, dst = ins[small + g], outs[small + g]
+            count = weights[g] // 4
+            halves = split_rows(count)
+
+            def rows(quarter, part=None):
+                start = pl.multiple_of(quarter * count, 16)
+                if part is None:
+                    return pl.ds(start, count)
+                return pl.ds(pl.multiple_of(start + part * halves[0], 16), halves[part])
+
+            return src, dst, rows
+
+        def z_sends(g):
+            src, dst, rows = plan(g)
+            copies = []
+            for k in range(1, 4):
+                peer = (c + k) % 4
+                copy = remote(
+                    src.at[rows(p)],
+                    dst.at[c, rows(p), lanes],
+                    wsend.at[g, k - 1],
+                    wrecv.at[g, 3 - k],
+                    (p, r, peer),
+                )
+                copy.start()
+                copies.append(copy)
+            copy = remote(src, dst.at[c, :, lanes], wsend.at[g, 3], wrecv.at[g, 3], twin)
+            copy.start()
+            copies.append(copy)
+            keep(src, dst.at[c, :, lanes], small + g)
+            return copies
+
+        def forward(g, block, quarter, part, slot, device):
+            _, dst, rows = plan(g)
+            view = dst.at[block, rows(quarter, part), lanes]
+            copy = remote(view, view, wsend.at[g, slot], wrecv.at[g, slot], device)
+            copy.start()
+            sent.append(copy)
+
+        def arrived(g, block, quarter, part, slot, which):
+            _, dst, rows = plan(g)
+            view = dst.at[block, rows(quarter, part), which]
+            remote(view, view, wsend.at[g, slot], wrecv.at[g, slot], twin).wait_recv()
+
+        x_dev, y_dev = (px, r, c), (py, r, c)
+        order = (1, 3, 2)
+        diag = 3 - p
+
+        def stage_plane(g):
+            for k in order:
+                block, base = (c + k) % 4, 4 + 9 * (k - 1)
+                arrived(g, block, p, None, k - 1, lanes)
+                forward(g, block, p, None, base, x_dev)
+                forward(g, block, p, None, base + 1, y_dev)
+                forward(g, block, p, None, base + 2, twin)
+
+        def stage_relay(g):
+            for k in order:
+                block, base = (c + k) % 4, 4 + 9 * (k - 1)
+                arrived(g, block, px, None, base, lanes)
+                forward(g, block, px, 0, base + 3, y_dev)
+                forward(g, block, px, None, base + 4, twin)
+                arrived(g, block, py, None, base + 1, lanes)
+                forward(g, block, py, 1, base + 5, x_dev)
+                forward(g, block, py, None, base + 6, twin)
+
+        def stage_last(g):
+            for k in order:
+                block, base = (c + k) % 4, 4 + 9 * (k - 1)
+                arrived(g, block, diag, 0, base + 3, lanes)
+                forward(g, block, diag, 0, base + 7, twin)
+                arrived(g, block, diag, 1, base + 5, lanes)
+                forward(g, block, diag, 1, base + 8, twin)
+
+        count = len(weights)
+        pending = z_sends(0)
+        for step in range(count + 2):
+            if step < count:
+                for copy in pending:
+                    copy.wait_send()
+                if step + 1 < count:
+                    pending = z_sends(step + 1)
+                stage_plane(step)
+            if 0 <= step - 1 < count:
+                stage_relay(step - 1)
+            if 0 <= step - 2 < count:
+                stage_last(step - 2)
+
+        for index in range(small):
+            for k in range(1, 4):
+                view = outs[index].at[(c + k) % 4]
+                remote(view, view, zsend.at[index, k - 1], zrecv.at[index, k - 1], twin).wait_recv()
+        for g in range(count):
+            _, dst, rows = plan(g)
+            view = dst.at[c, :, other_lanes]
+            remote(view, view, wsend.at[g, 3], wrecv.at[g, 3], twin).wait_recv()
+            for k in order:
+                block, base = (c + k) % 4, 4 + 9 * (k - 1)
+                arrived(g, block, p, None, base + 2, other_lanes)
+                arrived(g, block, px, None, base + 4, other_lanes)
+                arrived(g, block, py, None, base + 6, other_lanes)
+                arrived(g, block, diag, 0, base + 7, other_lanes)
+                arrived(g, block, diag, 1, base + 8, other_lanes)
+        for copy in sent:
+            copy.wait_send()
+        for copy in locals_:
+            copy.wait()
+
+    return kernel
+
+
+def gather_all(swaps, casts, weights):
+    args = (*swaps, *casts, *weights)
+    outs = [jax.ShapeDtypeStruct(a.shape, a.dtype) for a in swaps]
+    outs += [jax.ShapeDtypeStruct((4,) + a.shape, a.dtype) for a in casts]
+    outs += [jax.ShapeDtypeStruct((4, a.shape[0], 2 * HALF), a.dtype) for a in weights]
+    small = len(swaps) + len(casts)
+    dma = pltpu.SemaphoreType.DMA
+    return comm_call(
+        gather_kernel(swaps, casts, [a.shape[0] for a in weights]),
+        args,
+        outs,
+        [
+            dma((small, 3)),
+            dma((small, 3)),
+            dma((len(weights), 31)),
+            dma((len(weights), 31)),
+            dma((small + len(weights),)),
+        ],
+        1,
+    )
+
+
+def plane_kernel(number):
+    def kernel(*refs):
+        ins, outs = refs[:number], refs[number : 2 * number]
+        send_sem, recv_sem, local_sem = refs[2 * number :]
+        p, r, c = position()
+        greet([((p + k) % 4, r, c) for k in range(1, 4)])
+        copies, owns = [], []
+        for index in range(number):
+            for k in (2, 1, 3):
+                peer = (p + k) % 4
+                copy = remote(
+                    ins[index].at[peer],
+                    outs[index].at[p],
+                    send_sem.at[index, k - 1],
+                    recv_sem.at[index, 3 - k],
+                    (peer, r, c),
+                )
+                copy.start()
+                copies.append(copy)
+            own = pltpu.make_async_copy(
+                ins[index].at[p], outs[index].at[p], local_sem.at[index]
+            )
+            own.start()
+            owns.append(own)
+        for index in range(number):
+            for k in range(1, 4):
+                view = outs[index].at[(p + k) % 4]
+                remote(
+                    view, view, send_sem.at[index, k - 1], recv_sem.at[index, k - 1], (p, 1 - r, c)
+                ).wait_recv()
+        for copy in copies:
+            copy.wait_send()
+        for own in owns:
+            own.wait()
+
+    return kernel
+
+
+def plane_swap(args, ident):
+    dma = pltpu.SemaphoreType.DMA
+    number = len(args)
+    return comm_call(
+        plane_kernel(number),
+        args,
+        [jax.ShapeDtypeStruct(a.shape, a.dtype) for a in args],
+        [dma((number, 3)), dma((number, 3)), dma((number,))],
+        ident,
+    )
+
 
 D = 768
 HDIM = 64
@@ -407,6 +687,313 @@
     )
 
 
+def dot_at(left, right, contract):
+    return lax.dot_general(
+        left, right, (contract, ((), ())), preferred_element_type=jnp.float32
+    )
+
+
+NN = ((1,), (0,))
+NT = ((1,), (1,))
+TN = ((0,), (0,))
+
+
+def wide(ref):
+    return jnp.concatenate([ref[block] for block in range(ref.shape[0])], axis=1)
+
+
+def attend_kernel(q_ref, k_ref, v_ref, o_ref, low_ref, p_ref, inv_ref):
+    keys = wide(k_ref)
+    values = wide(v_ref)
+    for block in range(q_ref.shape[0]):
+        query = q_ref[block]
+        scores = dot_at(keys, query, TN) * 0.125
+        exps = jnp.exp(scores - jnp.max(scores, axis=0, keepdims=True))
+        inverse = 1.0 / jnp.sum(exps, axis=0, keepdims=True)
+        low = exps.astype(jnp.bfloat16)
+        p_ref[0, block] = low
+        inv_ref[0, block] = inverse
+        out = dot_at(values, low, NN) * inverse
+        o_ref[block] = out
+        low_ref[block] = out.astype(jnp.bfloat16)
+
+
+def attend(qkv):
+    blocks, _, width = qkv.shape
+    heads = qkv.shape[1] // 192
+
+    def part(offset):
+        return pl.BlockSpec((blocks, 64, width), lambda h: (0, h + offset * heads, 0))
+
+    total = blocks * width
+    return pl.pallas_call(
+        attend_kernel,
+        grid=(heads,),
+        out_shape=[
+            jax.ShapeDtypeStruct((blocks, 64 * heads, width), jnp.float32),
+            jax.ShapeDtypeStruct((blocks, 64 * heads, width), jnp.bfloat16),
+            jax.ShapeDtypeStruct((heads, blocks, total, width), jnp.bfloat16),
+            jax.ShapeDtypeStruct((heads, blocks, 1, width), jnp.float32),
+        ],
+        in_specs=[part(0), part(1), part(2)],
+        out_specs=[
+            part(0),
+            part(0),
+            pl.BlockSpec((1, blocks, total, width), lambda h: (h, 0, 0, 0)),
+            pl.BlockSpec((1, blocks, 1, width), lambda h: (h, 0, 0, 0)),
+        ],
+        compiler_params=pltpu.CompilerParams(vmem_limit_bytes=VMEM_GRANT),
+    )(qkv, qkv, qkv)
+
+
+def attend_back_kernel(q_ref, k_ref, v_ref, d_ref, o_ref, p_ref, inv_ref, dq_ref, dk_ref, dv_ref):
+    keys = wide(k_ref)
+    values = wide(v_ref)
+    width = q_ref.shape[2]
+    dkeys = jnp.zeros(keys.shape, jnp.float32)
+    dvalues = jnp.zeros(keys.shape, jnp.float32)
+    for block in range(q_ref.shape[0]):
+        query = q_ref[block]
+        grad = d_ref[block].astype(jnp.float32)
+        inverse = inv_ref[0, block]
+        delta = jnp.sum(grad * o_ref[block], axis=0, keepdims=True) * inverse
+        scaled = (grad * inverse).astype(jnp.bfloat16)
+        low = p_ref[0, block]
+        dprobs = dot_at(values, scaled, TN)
+        dscores = (low.astype(jnp.float32) * (dprobs - delta)).astype(jnp.bfloat16)
+        dq_ref[block] = (dot_at(keys, dscores, NN) * 0.125).astype(jnp.bfloat16)
+        dkeys = dkeys + dot_at(query, dscores, NT)
+        dvalues = dvalues + dot_at(scaled, low, NT)
+    for block in range(q_ref.shape[0]):
+        span = slice(block * width, (block + 1) * width)
+        dk_ref[block] = (dkeys[:, span] * 0.125).astype(jnp.bfloat16)
+        dv_ref[block] = dvalues[:, span].astype(jnp.bfloat16)
+
+
+def attend_back(qkv, grad, out, probs, inverse):
+    blocks, _, width = qkv.shape
+    heads = qkv.shape[1] // 192
+
+    def part(offset):
+        return pl.BlockSpec((blocks, 64, width), lambda h: (0, h + offset * heads, 0))
+
+    total = blocks * width
+    piece = jax.ShapeDtypeStruct((blocks, 64 * heads, width), jnp.bfloat16)
+    return pl.pallas_call(
+        attend_back_kernel,
+        grid=(heads,),
+        out_shape=[piece, piece, piece],
+        in_specs=[
+            part(0),
+            part(1),
+            part(2),
+            part(0),
+            part(0),
+            pl.BlockSpec((1, blocks, total, width), lambda h: (h, 0, 0, 0)),
+            pl.BlockSpec((1, blocks, 1, width), lambda h: (h, 0, 0, 0)),
+        ],
+        out_specs=[part(0), part(0), part(0)],
+        compiler_params=pltpu.CompilerParams(vmem_limit_bytes=VMEM_GRANT),
+    )(qkv, qkv, qkv, grad, out, probs, inverse)
+
+
+def pool_exchange(part):
+    return plane_swap((jnp.broadcast_to(part[None], (4,) + part.shape),), 3)[0]
+
+
+def layer_norm_rows(hidden, gain_vec, shift_vec):
+    average = jnp.mean(hidden, axis=1, keepdims=True)
+    spread = jnp.mean(hidden * hidden, axis=1, keepdims=True) - average * average
+    inv_std = lax.rsqrt(spread + eps_norm)
+    centred = (hidden - average) * inv_std
+    return (centred * gain_vec + shift_vec, centred, inv_std)
+
+
+def layer_norm_back(upstream, centred, inv_std, gain_vec):
+    scaled = upstream * gain_vec
+    return inv_std * (
+        scaled
+        - jnp.mean(scaled, axis=1, keepdims=True)
+        - centred * jnp.mean(scaled * centred, axis=1, keepdims=True)
+    )
+
+
+def quad_body(
+    tokens,
+    cotangent,
+    labels,
+    q_weight,
+    k_weight,
+    v_weight,
+    out_weight,
+    up_weight,
+    down_weight,
+    ln1_gain,
+    ln1_bias,
+    ln2_gain,
+    ln2_bias,
+    cls_in,
+    pool_query,
+    cls_mid,
+    cls_out,
+):
+    low = jnp.bfloat16
+    rows_here = tokens.shape[2]
+    pool_dim = CLS_D // POOL_HEADS
+    pool_root = math.sqrt(pool_dim)
+    qkv_shard = jnp.concatenate([q_weight.T, k_weight.T, v_weight.T], axis=0)
+    norm_shard = jnp.pad(
+        jnp.stack([ln1_gain, ln1_bias, ln2_gain, ln2_bias]), ((0, 4), (0, 64))
+    )
+    x4, cot4, norms4, cls4, w_qkv, w_out, w_up, w_down = gather_all(
+        (tokens[:, 0], cotangent[:, 0]),
+        (norm_shard, cls_in),
+        (qkv_shard, out_weight, up_weight.T, down_weight),
+    )
+    inputs = jnp.transpose(x4, (1, 0, 2)).reshape(rows_here, D)
+    cot = jnp.transpose(cot4, (1, 0, 2)).reshape(rows_here, D)
+    norms = jnp.transpose(norms4[:, :4, :192], (1, 0, 2)).reshape(4, D)
+    gain_one, bias_one, gain_two, bias_two = (norms[i][None] for i in range(4))
+    cls_full = cls4.reshape(D, CLS_D)
+    w_qkv, w_out, w_up, w_down = (w.reshape(-1, D) for w in (w_qkv, w_out, w_up, w_down))
+
+    qkv = dot_at(w_qkv, inputs, NT).astype(low).reshape(4, 576, rows_here)
+    qkv = plane_swap((qkv,), 2)[0]
+    attended, attended_heads, probs, inverse = attend(qkv)
+    attended_low = plane_swap((attended_heads,), 4)[0].reshape(D, rows_here)
+    branch = dot_at(attended_low, w_out, TN)
+    normed, centred_one, inv_one = layer_norm_rows(
+        inputs.astype(jnp.float32) + branch, gain_one, bias_one
+    )
+    normed_low = normed.astype(low)
+    up_pre = dot_at(w_up, normed_low, NT)
+    activated, gelu_back = jax.vjp(exact_gelu, up_pre)
+    activated_low = activated.astype(low)
+    down_out = dot_at(activated_low, w_down, TN)
+    outputs, centred_two, inv_two = layer_norm_rows(normed + down_out, gain_two, bias_two)
+    outputs_low = outputs.astype(low)
+    cls_proj = jnp.dot(outputs_low, cls_full, preferred_element_type=jnp.float32)
+    pool_heads = cls_proj.reshape(rows_here, POOL_HEADS, pool_dim)
+    pool_scores = jnp.einsum("lpd,pd->lp", pool_heads, pool_query, precision=highest) / pool_root
+    local_top = jnp.max(pool_scores, axis=0)
+    pool_exp = jnp.exp(pool_scores - local_top)
+    stats = jnp.stack(
+        [
+            jnp.repeat(local_top, pool_dim),
+            jnp.repeat(jnp.sum(pool_exp, axis=0), pool_dim),
+            jnp.einsum("lp,lpd->pd", pool_exp, pool_heads, precision=highest).reshape(CLS_D),
+        ]
+    )
+    stats = pool_exchange(jnp.pad(stats, ((0, 5), (0, 0))))
+    joint_top = jnp.max(stats[:, 0], axis=0)
+    rescale = jnp.exp(stats[:, 0] - joint_top)
+    joint_total = jnp.sum(stats[:, 1] * rescale, axis=0)
+    pooled_row = (jnp.sum(stats[:, 2] * rescale, axis=0) / joint_total)[None]
+    pooled = pooled_row.reshape(POOL_HEADS, pool_dim)
+    pool_weights = jnp.exp(pool_scores - joint_top[::pool_dim]) / joint_total[::pool_dim]
+    hidden_cls = jnp.tanh(jnp.dot(pooled_row, cls_mid, precision=highest))
+    logits = jnp.dot(hidden_cls, cls_out, precision=highest)[0]
+    col = lax.axis_index("cols")
+    label = lax.dynamic_index_in_dim(labels[:, 0], col, 0, False)
+    target_hit = lax.iota(jnp.int32, CLASSES) == label
+    loss = jax.nn.logsumexp(logits) - jnp.sum(jnp.where(target_hit, logits, 0.0))
+    dlogits = jax.nn.softmax(logits) - target_hit.astype(jnp.float32)
+    grad_top = hidden_cls[0][:, None] * dlogits[None, :]
+    dhidden = jnp.dot(cls_out, dlogits, precision=highest)
+    dpre_tanh = dhidden * (1.0 - hidden_cls[0] * hidden_cls[0])
+    grad_mid = pooled_row[0][:, None] * dpre_tanh[None, :]
+    dpooled = jnp.dot(cls_mid, dpre_tanh, precision=highest).reshape(POOL_HEADS, pool_dim)
+    dweights = jnp.einsum("lpd,pd->lp", pool_heads, dpooled, precision=highest)
+    dpool_scores = pool_weights * (dweights - jnp.sum(pooled * dpooled, axis=1))
+    dheads = (
+        pool_weights[:, :, None] * dpooled[None]
+        + dpool_scores[:, :, None] * (pool_query / pool_root)[None]
+    )
+    grad_pool = jnp.einsum("lp,lpd->pd", dpool_scores, pool_heads, precision=highest) / pool_root
+    dproj_low = dheads.reshape(rows_here, CLS_D).astype(low)
+    grad_cls_in = dot_rows(outputs_low, dproj_low)
+    upstream = cot.astype(jnp.float32) + dot_cols(dproj_low, cls_full)
+    sums = [jnp.sum(upstream * centred_two, axis=0), jnp.sum(upstream, axis=0)]
+    dhidden_two = layer_norm_back(upstream, centred_two, inv_two, gain_two)
+    ddown = dhidden_two.astype(low)
+    g_down = dot_at(activated_low, ddown, NN).astype(low)
+    dup = gelu_back(dot_at(w_down, ddown, NT))[0].astype(low)
+    g_up = dot_at(dup, normed_low, NN).astype(low)
+    dnormed = dhidden_two + dot_at(dup, w_up, TN)
+    sums += [jnp.sum(dnormed * centred_one, axis=0), jnp.sum(dnormed, axis=0)]
+    dhidden_one = layer_norm_back(dnormed, centred_one, inv_one, gain_one)
+    dbranch = dhidden_one.astype(low)
+    g_out = dot_at(attended_low, dbranch, NN).astype(low)
+    dattended = dot_at(w_out, dbranch, NT).astype(low).reshape(4, 192, rows_here)
+    dattended = plane_swap((dattended,), 5)[0]
+    dqkv = jnp.concatenate(attend_back(qkv, dattended, attended, probs, inverse), axis=1)
+    dqkv = plane_swap((dqkv,), 6)[0].reshape(4 * 576, rows_here)
+    g_qkv = dot_at(dqkv, inputs, NN).astype(low)
+    grad_inputs = dhidden_one + dot_at(dqkv, w_qkv, TN)
+
+    lead = (lax.axis_index("dp") == 0).astype(jnp.float32)
+    slot = lax.axis_index("rows") * 4 + col
+    loss_row = jnp.where(lax.iota(jnp.int32, CLS_D) == slot, loss * lead, 0.0)
+    packed = jnp.concatenate(
+        [
+            grad_cls_in,
+            jnp.stack(sums).reshape(4 * D // CLS_D, CLS_D),
+            grad_mid * lead,
+            grad_top.T * lead,
+            grad_pool.reshape(1, CLS_D),
+            loss_row[None],
+        ],
+        axis=0,
+    )
+    packed = lax.psum(packed, ("dp", "rows", "cols"))
+    sum_cls_in = lax.dynamic_slice_in_dim(packed[:D], col * 192, 192, 0)
+    norm_sums = lax.dynamic_slice_in_dim(packed[D : D + 24].reshape(4, D), col * 192, 192, 1)
+    at = D + 24
+    sum_mid = packed[at : at + CLS_D]
+    sum_top = packed[at + CLS_D : at + CLS_D + CLASSES].T
+    sum_pool = packed[at + CLS_D + CLASSES].reshape(POOL_HEADS, pool_dim)
+    losses = lax.dynamic_slice_in_dim(packed[at + CLS_D + CLASSES + 1], (slot - col), 4, 0)
+
+    def features_out(value):
+        blocks = jnp.transpose(value.reshape(rows_here, 4, 192), (1, 0, 2))
+        return blocks
+
+    out_blocks, grad_blocks, r_qkv, r_out, r_up, r_down = reduce_all(
+        (features_out(outputs_low), features_out(grad_inputs.astype(low))),
+        (g_qkv, g_out, g_up, g_down),
+    )
+    wide_ = jnp.float32
+    return (
+        out_blocks[:, None],
+        losses[:, None],
+        grad_blocks.astype(wide_)[:, None],
+        r_qkv[:192].T.astype(wide_),
+        r_qkv[192:384].T.astype(wide_),
+        r_qkv[384:].T.astype(wide_),
+        r_out.astype(wide_),
+        r_up.T.astype(wide_),
+        r_down.astype(wide_),
+        norm_sums[2],
+        norm_sums[3],
+        norm_sums[0],
+        norm_sums[1],
+        sum_cls_in,
+        sum_pool,
+        sum_mid,
+        sum_top,
+    )
+
+
+def reduce_all(swaps, grads):
+    moved = [lax.all_to_all(a, "cols", 0, 0, tiled=True) for a in swaps]
+    done = []
+    for grad in grads:
+        part = lax.psum_scatter(grad, "rows", scatter_dimension=1, tiled=True)
+        part = lax.psum_scatter(part, "cols", scatter_dimension=0, tiled=True)
+        done.append(lax.psum(part, "dp"))
+    return (*moved, *done)
+
+
 def solution(mesh):
     placed = (
         P(None, "rows", "dp", "cols"),
@@ -427,8 +1014,9 @@
         P(),
         P(),
     )
+    even = dict(mesh.shape) == {"dp": 4, "rows": 2, "cols": 4}
     return jax.shard_map(
-        body,
+        quad_body if even else body,
         mesh=mesh,
         in_specs=placed,
         out_specs=(

time: 1270 us -> 596 us (0.47); the launches traced: 1250 us -> 593 us
  blocking collectives: 458 us -> 0 us
  Pallas kernels: 0 us -> 171 us
  other arithmetic: 144 us -> 17.9 us
  matrix products: 158 us -> 49.7 us
  waiting for transfers between devices: 364 us -> 257 us
  local copies, waits for them, and re-layouts: 96.8 us -> 71.1 us
    all_gather x28 -> x0, blocking collectives: 343 us -> none  [the longest x16 244 us: features(): return lax.all_gather(shard_part, 'cols', axis=1, tiled=True)]
    pallas_call x0 -> x8, Pallas kernels: none -> 171 us  [the longest x6 147 us: comm_call(): pl.pallas_call(kernel, out_shape=outs, in_specs=[any_spec] * len(args), o...]
    psum x8 -> x0, blocking collectives: 95.4 us -> none  [the longest x7 69.3 us: token_sums(): return lax.psum((plain_sum, cross_sum), 'cols')]
    psum x4 -> x2, waiting for transfers between devices: 148 us -> 85.5 us  [the longest x1 58.4 us: reduce_all(): done.append(lax.psum(part, 'dp'))]
    dot_general x76 -> x21, matrix products: 101 us -> 48.8 us  [the longest x12 46.5 us: dot_at(): lax.dot_general(left, right, (contract, ((), ())), preferred_element_type...]
    reduce_scatter x21 -> x4, waiting for transfers between devices: 195 us -> 154 us  [reduce_all(): part = lax.psum_scatter(part, 'cols', scatter_dimension=0, tiled=True)]
    add x37 -> x0, other arithmetic: 38 us -> none  [the longest x12 15.9 us: pool_combine(): sum_left * scale_left[:, None] + sum_right * scale_right[:, None]]
    reduce_sum x23 -> x4, other arithmetic: 38.2 us -> 2.23 us  [the longest x1 1.9 us: quad_body(): jnp.sum(jnp.where(target_hit, logits, 0.0))]
  transfers between devices with their start and end apart: 32 -> 12, of which waited for: 17 -> 8; matrix products, arithmetic and copies ran while one was open for 15% -> 12% of each run, Pallas kernels for 0% -> 5%
where the time goes in v1:
time: 596 us; the launch traced here: 593 us
  waiting for transfers between devices  257 us (43%)
  Pallas kernels  171 us (29%)
  local copies, waits for them, and re-layouts  71.1 us (12%)
  matrix products  49.7 us (8%)
  between operations  18.9 us (3%)
  other arithmetic  17.9 us (3%)
  starting transfers between devices  7.34 us (1%)
    reduce_scatter x4, waiting for transfers between devices, reduce_all(): part = lax.psum_scatter(part, 'cols', scatter_dimension=0, tiled=True)  154 us
    pallas_call x6, Pallas kernels, comm_call(): pl.pallas_call(kernel, out_shape=outs, in_specs=[any_spec] * len(args), o...  147 us
    psum x1, waiting for transfers between devices, reduce_all(): done.append(lax.psum(part, 'dp'))  58.4 us
    unnamed x65, local copies, waits for them, and re-layouts  48.3 us
    dot_general x12, matrix products, dot_at(): lax.dot_general(left, right, (contract, ((), ())), preferred_element_type...  46.5 us
    psum x1, waiting for transfers between devices, quad_body(): packed = lax.psum(packed, ('dp', 'rows', 'cols'))  27.1 us
    pallas_call x1, Pallas kernels, attend(): pl.pallas_call(attend_kernel, grid=(heads,), out_shape=[jax.ShapeDtypeStr...  12.1 us
  transfers between devices with their start and end apart: 12, of which 8 were waited for; matrix products, arithmetic and copies ran while one was open for 12% of the time, Pallas kernels for 5%

profile of v1, /device:TPU:0, one launch (start us, length us, event | category | flops | bytes accessed | tf_op | source)
XLA Modules:
  0.0 593.5 jit_solution(18277472257125134165)
XLA Ops:
  17.4 96.3 %shard_map.296 = (bf16[4,256,192]{2,1,0:T(8,128)(2,1)}, bf16[4,256,192]{2,1,0:T(8,128)(2,1)}, f32[4,8,256]{2,1,0:T(8,128)}, bf16[4,192,128]{2,1,0:T(8,128)(2,1)}...) custom-call(bf16[4,256,192]{2,1,0:T(8,128)(2,1)} %bitcast.204, ...), custom_call_target="tpu_custom_call" | custom-call | tf_op jit(solution)/shard_map/pallas_call | solution.py:52
  117.4 4.1 convolution_convert_fusion.3
  121.5 18.4 %shard_map.297.q_ref.k_ref.v_ref = bf16[4,576,256]{2,1,0:T(8,128)(2,1)} custom-call(bf16[4,576,256]{2,1,0:T(8,128)(2,1)} %bitcast.211), custom_call_target="tpu_custom_call" | custom-call | tf_op jit(solution)/shard_map/pallas_call | solution.py:52
  139.9 12.1 %shard_map.298 = (f32[4,192,256]{2,1,0:T(8,128)}, bf16[4,192,256]{2,1,0:T(8,128)(2,1)}, bf16[3,4,1024,256]{3,2,1,0:T(8,128)(2,1)}, f32[3,4,1,256]{3,2,1,0:T(1,128)}) custom-call(bf16[4,576,256]{2,1,0:T(8,128)(2,1)} %shard_map.297.q_ref.k_ref.v_ref, bf16[4,576,256]{2,1,0:T(8,128)(2,1)} %shard_map.297.q_ref.k_ref.v_ref, ...), custom_call_target="tpu_custom_call" | custom-call | tf_op jit(solution)/shard_map/pallas_call | solution.py:729
  152.1 7.8 %shard_map.299 = bf16[4,192,256]{2,1,0:T(8,128)(2,1)} custom-call(bf16[4,192,256]{2,1,0:T(8,128)(2,1)} %get-tuple-element.34.refs_0_), custom_call_target="tpu_custom_call" | custom-call | tf_op jit(solution)/shard_map/pallas_call | solution.py:52
  161.7 11.4 %multiply_convert_fusion = (bf16[3072,256]{1,0:T(8,128)(2,1)S(1)}, f32[3072,256]{1,0:T(8,128)}, f32[3072,256]{1,0:T(8,128)}) fusion(bf16[3072,768]{1,0:T(8,128)(2,1)} %bitcast.239, f32[256,768]{1,0:T(8,128)S(1)} %get-tuple-element.145, f32[768]{0:T(1024)S(1)} %add.113, f32[768]{0:T(1024)S(1)} %mul.267, f32[256]{0:T(256)S(1)} %get-tuple-element.144, ...), kind=kOutput, calls=%fused_computation.7 | convolution fusion | flops 1260060672 | bytes 13377536 | tf_op jit(solution)/shard_map/dot_general | solution.py:691
  177.1 4.9 shard_map.300
  196.0 5.9 %add_convert_fusion = bf16[3072,256]{1,0:T(8,128)(2,1)S(1)} fusion(f32[3072,256]{1,0:T(8,128)S(1)} %copy-done.21, f32[3072,256]{1,0:T(8,128)} %get-tuple-element.146, bf16[3072,768]{1,0:T(8,128)(2,1)} %bitcast.243, f32[256,768]{1,0:T(8,128)S(1)} %subtract_multiply_fusion.1), kind=kOutput, calls=%fused_computation.6 | convolution fusion | flops 1219166208 | bytes 13369344 | tf_op jit(solution)/shard_map/dot_general | solution.py:691
  208.6 7.0 %shard_map.301.d_ref = bf16[4,192,256]{2,1,0:T(8,128)(2,1)} custom-call(bf16[4,192,256]{2,1,0:T(8,128)(2,1)} %bitcast.209), custom_call_target="tpu_custom_call" | custom-call | tf_op jit(solution)/shard_map/pallas_call | solution.py:52
  215.5 11.7 %shard_map.302 = (bf16[4,192,256]{2,1,0:T(8,128)(2,1)}, bf16[4,192,256]{2,1,0:T(8,128)(2,1)}, bf16[4,192,256]{2,1,0:T(8,128)(2,1)}) custom-call(bf16[4,576,256]{2,1,0:T(8,128)(2,1)} %shard_map.297.q_ref.k_ref.v_ref, bf16[4,576,256]{2,1,0:T(8,128)(2,1)} %shard_map.297.q_ref.k_ref.v_ref, bf16[4,576,256]{2,1,0:T(8,128)(2,1)} %shard_map.297.q_ref.k_ref.v_ref, ...), custom_call_target="tpu_custom_call" | custom-call | tf_op jit(solution)/shard_map/pallas_call | solution.py:782
  229.5 13.0 %shard_map.303 = bf16[4,576,256]{2,1,0:T(8,128)(2,1)} custom-call(bf16[4,576,256]{2,1,0:T(8,128)(2,1)} %pad_maximum_fusion.refs_0_), custom_call_target="tpu_custom_call" | custom-call | tf_op jit(solution)/shard_map/pallas_call | solution.py:52
  242.5 4.2 convolution_convert_fusion.2
  246.7 5.8 copy.83
  253.9 4.8 convolution_convert_fusion.1
  258.8 6.7 %copy.87 = bf16[3072,768]{0,1:T(8,128)(2,1)} copy(bf16[3072,768]{1,0:T(8,128)(2,1)} %convolution_convert_fusion.1) | data formatting | bytes 9437184
  267.0 4.8 convolution_convert_fusion
  271.8 7.0 %copy.89 = bf16[3072,768]{0,1:T(8,128)(2,1)} copy(bf16[3072,768]{1,0:T(8,128)(2,1)} %convolution_convert_fusion) | data formatting | bytes 9437184
  281.2 3.9 copy.84
  285.2 4.3 copy.88
  289.6 9.2 %reduce-scatter.31.cloned.1.call-done = bf16[384,3072]{1,0:T(8,128)(2,1)} async-done(((bf16[768,3072]{1,0:T(8,128)(2,1)}), bf16[384,3072]{1,0:T(8,128)(2,1)}) %reduce-scatter.31.cloned.1.call-update) | async-done | bytes 2359312
  298.8 4.3 copy.90
  305.7 3.9 concatenate.10
  309.7 15.5 %reduce-scatter.19.cloned.1.call-done = bf16[192,384]{1,0:T(8,128)(2,1)} async-done(((bf16[768,384]{1,0:T(8,128)(2,1)}), bf16[192,384]{1,0:T(8,128)(2,1)}) %reduce-scatter.19.cloned.1.call-update) | async-done | bytes 147472 | tf_op jit(solution)/shard_map/reduce_scatter | solution.py:992
  325.2 39.6 %reduce-scatter.17.cloned.1.call-done = bf16[576,384]{1,0:T(8,128)(2,1)} async-done(((bf16[2304,384]{1,0:T(8,128)(2,1)}), bf16[576,384]{1,0:T(8,128)(2,1)}) %reduce-scatter.17.cloned.1.call-update) | async-done | bytes 442384 | tf_op jit(solution)/shard_map/reduce_scatter | solution.py:992
  364.8 49.3 %reduce-scatter.21.cloned.1.call-done = bf16[768,384]{1,0:T(8,128)(2,1)} async-done(((bf16[3072,384]{1,0:T(8,128)(2,1)}), bf16[768,384]{1,0:T(8,128)(2,1)}) %reduce-scatter.21.cloned.1.call-update) | async-done | bytes 589840 | tf_op jit(solution)/shard_map/reduce_scatter | solution.py:992
  414.2 49.8 %reduce-scatter.23.cloned.1.call-done = bf16[768,384]{1,0:T(8,128)(2,1)} async-done(((bf16[3072,384]{1,0:T(8,128)(2,1)}), bf16[768,384]{1,0:T(8,128)(2,1)}) %reduce-scatter.23.cloned.1.call-update) | async-done | bytes 589840 | tf_op jit(solution)/shard_map/reduce_scatter | solution.py:992
  464.9 3.5 all-to-all-start
  468.4 3.1 fusion.8
  472.5 8.0 %all-to-all-done = bf16[4,256,192]{1,2,0:T(8,128)(2,1)S(1)} async-done(((bf16[4,256,192]{1,2,0:T(8,128)(2,1)}), bf16[4,256,192]{1,2,0:T(8,128)(2,1)S(1)}, u32[]{:S(2)}, u32[]{:S(2)}) %all-to-all-start) | async-done | bytes 393248 | tf_op jit(solution)/shard_map/all_to_all | solution.py:988
  480.5 3.5 all-to-all-start.1
  484.0 27.1 %all-reduce.6.cloned.1.call-done = f32[936,128]{1,0:T(8,128)} async-done(((f32[936,128]{1,0:T(8,128)}), f32[936,128]{1,0:T(8,128)}) %all-reduce.6.cloned.1.call-update) | async-done | bytes 479248 | tf_op jit(solution)/shard_map/psum | solution.py:948
  519.8 58.4 %all-reduce.8.cloned.1.call-done = (bf16[384,768]{0,1:T(8,128)(2,1)}, bf16[576,384]{1,0:T(8,128)(2,1)}, bf16[192,384]{1,0:T(8,128)(2,1)}, bf16[768,384]{1,0:T(8,128)(2,1)}) async-done(((bf16[384,768]{0,1:T(8,128)(2,1)}, bf16[576,384]{1,0:T(8,128)(2,1)}, bf16[192,384]{1,0:T(8,128)(2,1)}, bf16[768,384]{1,0:T(8,128)(2,1)}), (bf16[384,768]{0,1:T(8,128)(2,1)}, bf16[576,384]{1,0:T(8,128)(2,1)}, ...) | async-done | bytes 1769488 | tf_op jit(solution)/shard_map/psum | solution.py:993
  (178 shorter events, 65.0 us)
Async XLA Ops:
  8.0 175.2 %copy-start = (f32[128,128]{1,0:T(8,128)S(1)}, f32[128,128]{1,0:T(8,128)}, u32[]{:S(2)}) copy-start(f32[128,128]{1,0:T(8,128)} %param.32) | copy-start | bytes 196612
  8.0 8.8 %copy-start.16 = (f32[192]{0:T(256)S(1)}, f32[192]{0:T(256)}, u32[]{:S(2)}) copy-start(f32[192]{0:T(256)} %param.29) | copy-start | bytes 2308
  8.1 8.7 %copy-start.17 = (f32[192]{0:T(256)S(1)}, f32[192]{0:T(256)}, u32[]{:S(2)}) copy-start(f32[192]{0:T(256)} %param.28) | copy-start | bytes 2308
  8.1 8.7 %copy-start.18 = (f32[192]{0:T(256)S(1)}, f32[192]{0:T(256)}, u32[]{:S(2)}) copy-start(f32[192]{0:T(256)} %param.27) | copy-start | bytes 2308
  8.1 8.7 %copy-start.19 = (f32[192]{0:T(256)S(1)}, f32[192]{0:T(256)}, u32[]{:S(2)}) copy-start(f32[192]{0:T(256)} %param.26) | copy-start | bytes 2308
  8.1 270.8 %reduce-scatter.27.cloned.1.call-start = ((), (), s32[]{:S(2)}) async-start(), calls=%async_computation.16 | async-start | bytes 1769472
  121.5 38.4 %copy-start.11 = (bf16[4,192,768]{2,1,0:T(8,128)(2,1)S(1)}, bf16[4,192,768]{2,1,0:T(8,128)(2,1)}, u32[]{:S(2)}) copy-start(bf16[4,192,768]{2,1,0:T(8,128)(2,1)} %get-tuple-element.35) | copy-start | bytes 3538948
  159.9 13.3 %slice-start.2 = ((s8[4718592]{0:T(1024)(128)(4,1)}), s8[4194304]{0:T(1024)(128)(4,1)S(1)}, s32[]{:S(2)}) async-start(s8[4718592]{0:T(1024)(128)(4,1)} %bitcast.244), calls=%async_computation.22 | async-start | bytes 8388608
  161.7 11.5 %copy-start.8 = (f32[256,768]{1,0:T(8,128)}, f32[256,768]{1,0:T(8,128)S(1)}, u32[]{:S(2)}) copy-start(f32[256,768]{1,0:T(8,128)S(1)} %get-tuple-element.145) | copy-start | bytes 2359300
  161.7 11.5 %slice-start.3 = ((s8[4718592]{0:T(1024)(128)(4,1)}), s8[524288]{0:T(1024)(128)(4,1)S(1)}, s32[]{:S(2)}) async-start(s8[4718592]{0:T(1024)(128)(4,1)} %bitcast.244), calls=%async_computation.23 | async-start | bytes 1048576
  173.2 2.2 copy-start.15
  173.2 10.2 %copy-start.14 = (f32[128,14]{0,1:T(8,128)S(1)}, f32[128,14]{0,1:T(8,128)}, u32[]{:S(2)}) copy-start(f32[128,14]{0,1:T(8,128)} %param.33) | copy-start | bytes 21508
  173.2 11.6 %copy-start.20 = (s32[4,1]{0,1:T(1,128)S(1)}, s32[4,1]{0,1:T(1,128)}, u32[]{:S(2)}) copy-start(s32[4,1]{0,1:T(1,128)} %param.19) | copy-start | bytes 52
  175.0 19.6 %copy-start.12 = (bf16[4,192,128]{2,1,0:T(8,128)(2,1)S(1)}, bf16[4,192,128]{2,1,0:T(8,128)(2,1)}, u32[]{:S(2)}) copy-start(bf16[4,192,128]{2,1,0:T(8,128)(2,1)} %get-tuple-element.39) | copy-start | bytes 589828
  195.2 6.7 %slice-start = ((s8[4718592]{0:T(1024)(128)(4,1)}), s8[4194304]{0:T(1024)(128)(4,1)S(1)}, s32[]{:S(2)}) async-start(s8[4718592]{0:T(1024)(128)(4,1)} %bitcast.240), calls=%async_computation.20 | async-start | bytes 8388608
  195.5 6.5 %copy-start.7 = (f32[256,768]{1,0:T(8,128)}, f32[256,768]{1,0:T(8,128)S(1)}, u32[]{:S(2)}) copy-start(f32[256,768]{1,0:T(8,128)S(1)} %subtract_multiply_fusion.1) | copy-start | bytes 2359300
  196.0 6.0 %copy-start.9 = (f32[256,768]{1,0:T(8,128)S(1)}, f32[256,768]{1,0:T(8,128)}, u32[]{:S(2)}) copy-start(f32[256,768]{1,0:T(8,128)} %copy-done.8) | copy-start | bytes 2359300
  196.0 6.0 %slice-start.1 = ((s8[4718592]{0:T(1024)(128)(4,1)}), s8[524288]{0:T(1024)(128)(4,1)S(1)}, s32[]{:S(2)}) async-start(s8[4718592]{0:T(1024)(128)(4,1)} %bitcast.240), calls=%async_computation.21 | async-start | bytes 1048576
  206.0 75.2 %reduce-scatter.25.cloned.1.call-start = ((), (), s32[]{:S(2)}) async-start(), calls=%async_computation.15 | async-start | bytes 5308416
  252.5 32.7 %reduce-scatter.29.cloned.1.call-start = ((), (), s32[]{:S(2)}) async-start(), calls=%async_computation.17 | async-start | bytes 7077888
  265.5 33.3 %reduce-scatter.31.cloned.1.call-start = ((), (), s32[]{:S(2)}) async-start(), calls=%async_computation.18 | async-start | bytes 7077888
  278.8 46.4 %reduce-scatter.19.cloned.1.call-start = ((), (), s32[]{:S(2)}) async-start(), calls=%async_computation.12 | async-start | bytes 737280 | tf_op jit(solution)/shard_map/reduce_scatter | solution.py:992
  281.1 83.7 %reduce-scatter.17.cloned.1.call-start = ((), (), s32[]{:S(2)}) async-start(), calls=%async_computation.11 | async-start | bytes 2211840 | tf_op jit(solution)/shard_map/reduce_scatter | solution.py:992
  285.1 129.0 %reduce-scatter.21.cloned.1.call-start = ((), (), s32[]{:S(2)}) async-start(), calls=%async_computation.13 | async-start | bytes 2949120 | tf_op jit(solution)/shard_map/reduce_scatter | solution.py:992
  289.5 174.4 %reduce-scatter.23.cloned.1.call-start = ((), (), s32[]{:S(2)}) async-start(), calls=%async_computation.14 | async-start | bytes 2949120 | tf_op jit(solution)/shard_map/reduce_scatter | solution.py:992
  303.2 165.2 %copy-start.2 = (bf16[4,576,256]{2,1,0:T(8,128)(2,1)S(1)}, bf16[4,576,256]{2,1,0:T(8,128)(2,1)}, u32[]{:S(2)}) copy-start(bf16[4,576,256]{2,1,0:T(8,128)(2,1)} %shard_map.303) | copy-start | bytes 3538948
  303.2 207.8 %all-reduce.6.cloned.1.call-start = ((), (), s32[]{:S(2)}) async-start(), calls=%async_computation.10 | async-start | bytes 958464 | tf_op jit(solution)/shard_map/psum | solution.py:948
  309.7 268.5 %all-reduce.8.cloned.1.call-start = ((), (), s32[]{:S(2)}) async-start(), calls=%async_computation.19 | async-start | bytes 3538944 | tf_op jit(solution)/shard_map/psum | solution.py:993
  464.9 15.6 %all-to-all-start = ((bf16[4,256,192]{1,2,0:T(8,128)(2,1)}), bf16[4,256,192]{1,2,0:T(8,128)(2,1)S(1)}, u32[]{:S(2)}, u32[]{:S(2)}) async-start(bf16[4,256,192]{1,2,0:T(8,128)(2,1)} %bitcast.19), calls=%async_computation | async-start | bytes 786432 | tf_op jit(solution)/shard_map/all_to_all | solution.py:988
  480.5 38.4 %all-to-all-start.1 = ((bf16[4,256,192]{1,2,0:T(8,128)(2,1)}), bf16[4,256,192]{1,2,0:T(8,128)(2,1)S(1)}, u32[]{:S(2)}, u32[]{:S(2)}) async-start(bf16[4,256,192]{1,2,0:T(8,128)(2,1)} %bitcast.62), calls=%async_computation.1 | async-start | bytes 786432 | tf_op jit(solution)/shard_map/all_to_all | solution.py:988
  518.9 67.2 %copy-start.1 = (f32[128,128]{1,0:T(8,128)S(1)}, f32[128,128]{1,0:T(8,128)}, u32[]{:S(2)}) copy-start(f32[128,128]{1,0:T(8,128)} %param.32) | copy-start | bytes 196612
  578.2 6.0 %copy-start.13 = (bf16[768,384]{1,0:T(8,128)(2,1)S(1)}, bf16[768,384]{1,0:T(8,128)(2,1)}, u32[]{:S(2)}) copy-start(bf16[768,384]{1,0:T(8,128)(2,1)} %get-tuple-element.122) | copy-start | bytes 1769476
  (6 other events, 10.2 us)
Sparse Core Ops, SparseCore 0:
  206.1 10.4 reduce-scatter.26
  252.7 13.9 reduce-scatter.24
  268.9 13.8 reduce-scatter.28
  285.0 13.8 reduce-scatter.30
  301.5 23.6 reduce-scatter.18
  327.4 37.4 reduce-scatter.16
  367.1 46.9 reduce-scatter.20
  416.5 47.4 reduce-scatter.22
Sparse Core Ops, SparseCore 1:
  309.8 201.2 all-reduce.5
  514.4 63.8 all-reduce.7

commit v2 on v1

--- a/solution.py
+++ b/solution.py
@@ -984,14 +984,200 @@
     )
 
 
+def add_rows(dst, source, lead, start, count):
+    def one(block, unused):
+        spot = dst.at[lead(block), pl.ds(start, count)]
+        total = spot[...].astype(jnp.float32) + source(block)[...].astype(jnp.float32)
+        spot[...] = total.astype(jnp.bfloat16)
+        return unused
+
+    lax.fori_loop(0, 4, one, 0)
+
+
+def reduce_kernel(number, counts):
+    segs = len(counts)
+
+    def kernel(*refs):
+        swap_in, grads = refs[:number], refs[number : number + segs]
+        rest = refs[number + segs :]
+        swap_out, outs = rest[:number], rest[number : number + segs]
+        rest = rest[number + segs :]
+        acc, twin_buf, first_a, first_b, next_a, next_b, zbuf, final = (
+            rest[i * segs : (i + 1) * segs] for i in range(8)
+        )
+        ssend, srecv, send_sem, recv_sem, local_sem = rest[8 * segs :]
+        p, r, c = position()
+        px, py, diag = plane_x(p), plane_y(p), 3 - p
+        x_dev, y_dev, twin = (px, r, c), (py, r, c), (p, 1 - r, c)
+        greet([(p, r, (c + k) % 4) for k in range(1, 4)] + [x_dev, y_dev, twin])
+        sent, locals_ = [], []
+
+        def keep(src, dst, index):
+            copy = pltpu.make_async_copy(src, dst, local_sem.at[index])
+            copy.start()
+            return copy
+
+        def send(g, src, dst, slot, device):
+            copy = remote(src, dst, send_sem.at[g, slot], recv_sem.at[g, slot], device)
+            copy.start()
+            sent.append(copy)
+
+        def wait(g, view, slot):
+            remote(view, view, send_sem.at[g, slot], recv_sem.at[g, slot], twin).wait_recv()
+
+        lanes = pl.ds(pl.multiple_of(r * HALF, HALF), HALF)
+        other_lanes = pl.ds(pl.multiple_of((1 - r) * HALF, HALF), HALF)
+        mine = []
+        for g in range(segs):
+            send(g, grads[g].at[:, :, other_lanes], twin_buf[g], 0, twin)
+            mine.append(keep(grads[g].at[:, :, lanes], acc[g], g))
+        for index in range(number):
+            for k in range(1, 4):
+                peer = (c + k) % 4
+                copy = remote(
+                    swap_in[index].at[peer],
+                    swap_out[index].at[c],
+                    ssend.at[index, k - 1],
+                    srecv.at[index, 3 - k],
+                    (p, r, peer),
+                )
+                copy.start()
+                sent.append(copy)
+            locals_.append(keep(swap_in[index].at[c], swap_out[index].at[c], segs + index))
+
+        def span(g, quarter, part=None):
+            count = counts[g] // 4
+            halves = split_rows(count)
+            start = pl.multiple_of(quarter * count, 16)
+            if part is None:
+                return start, count
+            return pl.multiple_of(start + part * halves[0], 16), halves[part]
+
+        def cut(g, quarter, part=None):
+            return pl.ds(*span(g, quarter, part))
+
+        def same(block):
+            return block
+
+        def pair(g):
+            mine[g].wait()
+            wait(g, twin_buf[g], 0)
+
+            def one(index, unused):
+                block, step = index % 4, index // 4
+                part = pl.ds(pl.multiple_of(step * 48, 16), 48)
+                total = acc[g][block, part].astype(jnp.float32)
+                total = total + twin_buf[g][block, part].astype(jnp.float32)
+                acc[g][block, part] = total.astype(jnp.bfloat16)
+                return unused
+
+            lax.fori_loop(0, 4 * (counts[g] // 48), one, 0)
+            send(g, acc[g].at[:, cut(g, diag, 0)], first_a[g].at[1], 1, x_dev)
+            send(g, acc[g].at[:, cut(g, diag, 1)], first_b[g].at[1], 2, y_dev)
+            send(g, acc[g].at[:, cut(g, px, 0)], first_a[g].at[0], 3, x_dev)
+            send(g, acc[g].at[:, cut(g, py, 1)], first_b[g].at[0], 4, y_dev)
+
+        def second(g):
+            wait(g, first_a[g].at[1], 1)
+            add_rows(acc[g], lambda b: first_a[g].at[1, b], same, *span(g, py, 0))
+            send(g, acc[g].at[:, cut(g, py, 0)], next_a[g], 5, y_dev)
+            wait(g, first_b[g].at[1], 2)
+            add_rows(acc[g], lambda b: first_b[g].at[1, b], same, *span(g, px, 1))
+            send(g, acc[g].at[:, cut(g, px, 1)], next_b[g], 6, x_dev)
+            wait(g, first_a[g].at[0], 3)
+            add_rows(acc[g], lambda b: first_a[g].at[0, b], same, *span(g, p, 0))
+            wait(g, first_b[g].at[0], 4)
+            add_rows(acc[g], lambda b: first_b[g].at[0, b], same, *span(g, p, 1))
+
+        def third(g):
+            wait(g, next_a[g], 5)
+            add_rows(acc[g], lambda b: next_a[g].at[b], same, *span(g, p, 0))
+            wait(g, next_b[g], 6)
+            add_rows(acc[g], lambda b: next_b[g].at[b], same, *span(g, p, 1))
+            for k in (2, 1, 3):
+                peer = (c + k) % 4
+                copy = remote(
+                    acc[g].at[peer, cut(g, p)],
+                    zbuf[g].at[3 - k],
+                    send_sem.at[g, 6 + k],
+                    recv_sem.at[g, 10 - k],
+                    (p, r, peer),
+                )
+                copy.start()
+                sent.append(copy)
+
+        def fourth(g):
+            total = acc[g][c, cut(g, p)].astype(jnp.float32)
+            for k in range(3):
+                wait(g, zbuf[g].at[k], 7 + k)
+                total = total + zbuf[g][k].astype(jnp.float32)
+            final[g][cut(g, p)] = total.astype(jnp.bfloat16)
+            own = final[g].at[cut(g, p)]
+            send(g, own, own, 10, x_dev)
+            send(g, own, own, 11, y_dev)
+
+        def fifth(g):
+            wait(g, final[g].at[cut(g, px)], 10)
+            view = final[g].at[cut(g, px, 0)]
+            send(g, view, view, 12, y_dev)
+            wait(g, final[g].at[cut(g, py)], 11)
+            view = final[g].at[cut(g, py, 1)]
+            send(g, view, view, 13, x_dev)
+
+        def sixth(g):
+            wait(g, final[g].at[cut(g, diag, 0)], 12)
+            wait(g, final[g].at[cut(g, diag, 1)], 13)
+            locals_.append(keep(final[g], outs[g], segs + number + g))
+
+        stages = (pair, second, third, fourth, fifth, sixth)
+        for step in range(segs + len(stages) - 1):
+            for index, stage in enumerate(stages):
+                if 0 <= step - index < segs:
+                    stage(step - index)
+        for index in range(number):
+            for k in range(1, 4):
+                view = swap_out[index].at[(c + k) % 4]
+                remote(view, view, ssend.at[index, k - 1], srecv.at[index, k - 1], twin).wait_recv()
+        for copy in sent:
+            copy.wait_send()
+        for copy in locals_:
+            copy.wait()
+
+    return kernel
+
+
+def reduce_call(swaps, grads, ident):
+    low = jnp.bfloat16
+    grads = [g.reshape(4, -1, 2 * HALF) for g in grads]
+    counts = [g.shape[1] for g in grads]
+    halves = [split_rows(n // 4) for n in counts]
+    scratch = [pltpu.VMEM((4, n, HALF), low) for n in counts] * 2
+    scratch += [pltpu.VMEM((2, 4, h[0], HALF), low) for h in halves]
+    scratch += [pltpu.VMEM((2, 4, h[1], HALF), low) for h in halves]
+    scratch += [pltpu.VMEM((4, h[0], HALF), low) for h in halves]
+    scratch += [pltpu.VMEM((4, h[1], HALF), low) for h in halves]
+    scratch += [pltpu.VMEM((3, n // 4, HALF), low) for n in counts]
+    scratch += [pltpu.VMEM((n, HALF), low) for n in counts]
+    dma = pltpu.SemaphoreType.DMA
+    number, segs = len(swaps), len(counts)
+    scratch += [
+        dma((max(number, 1), 3)),
+        dma((max(number, 1), 3)),
+        dma((segs, 14)),
+        dma((segs, 14)),
+        dma((2 * segs + number,)),
+    ]
+    outs = [jax.ShapeDtypeStruct(a.shape, a.dtype) for a in swaps]
+    outs += [jax.ShapeDtypeStruct((n, HALF), low) for n in counts]
+    return comm_call(reduce_kernel(number, counts), (*swaps, *grads), outs, scratch, ident)
+
+
 def reduce_all(swaps, grads):
-    moved = [lax.all_to_all(a, "cols", 0, 0, tiled=True) for a in swaps]
-    done = []
-    for grad in grads:
-        part = lax.psum_scatter(grad, "rows", scatter_dimension=1, tiled=True)
-        part = lax.psum_scatter(part, "cols", scatter_dimension=0, tiled=True)
-        done.append(lax.psum(part, "dp"))
-    return (*moved, *done)
+    g_qkv, g_out, g_up, g_down = grads
+    moved_out, moved_in, r_down, r_up, r_out, r_qkv = reduce_call(
+        swaps, (g_down, g_up, g_out, g_qkv), 7
+    )
+    return (moved_out, moved_in, r_qkv, r_out, r_up, r_down)
 
 
 def solution(mesh):

time: 596 us -> 392 us (0.66)
  waiting for transfers between devices: 257 us -> 0.02 us
  Pallas kernels: 171 us -> 267 us
  local copies, waits for them, and re-layouts: 71.1 us -> 39.7 us
  starting transfers between devices: 7.34 us -> 0.04 us
    reduce_scatter x4 -> x0, waiting for transfers between devices: 154 us -> none  [reduce_all(): part = lax.psum_scatter(part, 'cols', scatter_dimension=0, tiled=True)]
    pallas_call x6 -> x7, Pallas kernels: 147 us -> 243 us  [comm_call(): pl.pallas_call(kernel, out_shape=outs, in_specs=[any_spec] * len(args), o...]
    psum x1 -> x0, waiting for transfers between devices: 58.4 us -> none  [reduce_all(): done.append(lax.psum(part, 'dp'))]
    unnamed x65 -> x108, local copies, waits for them, and re-layouts: 48.3 us -> 11.4 us
    psum x1, waiting for transfers between devices: 27.1 us -> 0.01 us  [quad_body(): packed = lax.psum(packed, ('dp', 'rows', 'cols'))]
    unnamed x14 -> x1, waiting for transfers between devices: 9.46 us -> 0.02 us
    all_to_all x2 -> x0, waiting for transfers between devices: 8.05 us -> none  [reduce_all(): moved = [lax.all_to_all(a, 'cols', 0, 0, tiled=True) for a in swaps]]
    all_to_all x2 -> x0, starting transfers between devices: 6.92 us -> none  [reduce_all(): moved = [lax.all_to_all(a, 'cols', 0, 0, tiled=True) for a in swaps]]
  transfers between devices with their start and end apart: 12 -> 1, of which waited for: 8 -> 0; matrix products, arithmetic and copies ran while one was open for 12% -> 9% of each run, Pallas kernels for 5% -> 33%
where the time goes in v2:
time: 392 us; the launch traced here: 390 us
  Pallas kernels  267 us (68%)
  matrix products  50.7 us (13%)
  local copies, waits for them, and re-layouts  39.7 us (10%)
  between operations  17.5 us (4%)
  other arithmetic  16 us (4%)
    pallas_call x7, Pallas kernels, comm_call(): pl.pallas_call(kernel, out_shape=outs, in_specs=[any_spec] * len(args), o...  243 us
    dot_general x12, matrix products, dot_at(): lax.dot_general(left, right, (contract, ((), ())), preferred_element_type...  45.9 us
    pallas_call x1, Pallas kernels, attend(): pl.pallas_call(attend_kernel, grid=(heads,), out_shape=[jax.ShapeDtypeStr...  12.1 us
    unnamed x108, local copies, waits for them, and re-layouts  11.4 us
    pallas_call x1, Pallas kernels, attend_back(): pl.pallas_call(attend_back_kernel, grid=(heads,), out_shape=[piece, piece...  11.4 us
  transfers between devices with their start and end apart: 1, of which 0 were waited for; matrix products, arithmetic and copies ran while one was open for 9% of the time, Pallas kernels for 33%

profile of v2, /device:TPU:0, one launch (start us, length us, event | category | flops | bytes accessed | tf_op | source)
XLA Modules:
  0.0 390.4 jit_solution(17233782381377493738)
XLA Ops:
  8.0 2.0 copy.45
  10.0 2.0 copy.46
  12.0 2.1 copy.47
  14.1 1.9 pad_maximum_fusion.1.refs_4_
  16.6 96.3 %shard_map.296 = (bf16[4,256,192]{2,1,0:T(8,128)(2,1)}, bf16[4,256,192]{2,1,0:T(8,128)(2,1)}, f32[4,8,256]{2,1,0:T(8,128)}, bf16[4,192,128]{2,1,0:T(8,128)(2,1)}...) custom-call(bf16[4,256,192]{2,1,0:T(8,128)(2,1)} %bitcast.192, ...), custom_call_target="tpu_custom_call" | custom-call | tf_op jit(solution)/shard_map/pallas_call | solution.py:52
  116.5 4.1 %convolution_convert_fusion.3 = bf16[2304,256]{1,0:T(8,128)(2,1)} fusion(bf16[2304,768]{1,0:T(8,128)(2,1)} %bitcast.189, bf16[256,768]{0,1:T(8,128)(2,1)S(1)} %bitcast.187), kind=kOutput, calls=%fused_computation.4 | convolution fusion | flops 906559488 | bytes 5111808 | tf_op jit(solution)/shard_map/dot_general | solution.py:691
  120.6 18.4 %shard_map.297.q_ref.k_ref.v_ref = bf16[4,576,256]{2,1,0:T(8,128)(2,1)} custom-call(bf16[4,576,256]{2,1,0:T(8,128)(2,1)} %bitcast.201), custom_call_target="tpu_custom_call" | custom-call | tf_op jit(solution)/shard_map/pallas_call | solution.py:52
  139.1 12.1 %shard_map.298 = (f32[4,192,256]{2,1,0:T(8,128)}, bf16[4,192,256]{2,1,0:T(8,128)(2,1)}, bf16[3,4,1024,256]{3,2,1,0:T(8,128)(2,1)}, f32[3,4,1,256]{3,2,1,0:T(1,128)}) custom-call(bf16[4,576,256]{2,1,0:T(8,128)(2,1)} %shard_map.297.q_ref.k_ref.v_ref, bf16[4,576,256]{2,1,0:T(8,128)(2,1)} %shard_map.297.q_ref.k_ref.v_ref, ...), custom_call_target="tpu_custom_call" | custom-call | tf_op jit(solution)/shard_map/pallas_call | solution.py:729
  151.2 7.8 %shard_map.299 = bf16[4,192,256]{2,1,0:T(8,128)(2,1)} custom-call(bf16[4,192,256]{2,1,0:T(8,128)(2,1)} %get-tuple-element.40.refs_0_), custom_call_target="tpu_custom_call" | custom-call | tf_op jit(solution)/shard_map/pallas_call | solution.py:52
  159.0 1.8 fusion.41
  160.9 11.5 %multiply_convert_fusion = (bf16[3072,256]{1,0:T(8,128)(2,1)S(1)}, f32[3072,256]{1,0:T(8,128)}, f32[3072,256]{1,0:T(8,128)}) fusion(bf16[3072,768]{1,0:T(8,128)(2,1)} %bitcast.228, f32[256,768]{1,0:T(8,128)S(1)} %get-tuple-element.136, f32[768]{0:T(1024)S(1)} %add.89, f32[768]{0:T(1024)S(1)} %mul.269, f32[256]{0:T(256)S(1)} %get-tuple-element.135, ...), kind=kOutput, calls=%fused_computation.7 | convolution fusion | flops 1260060672 | bytes 13377536 | tf_op jit(solution)/shard_map/dot_general | solution.py:691
  172.4 1.6 fusion.40
  176.7 4.9 %shard_map.300 = f32[4,8,128]{2,1,0:T(8,128)} custom-call(f32[4,8,128]{2,1,0:T(8,128)} %broadcast_in_dim.27.refs_0_), custom_call_target="tpu_custom_call" | custom-call | tf_op jit(solution)/shard_map/pallas_call | solution.py:52
  187.3 1.9 fusion.30
  189.2 1.9 divide_subtract_fusion
  200.4 5.5 %add_convert_fusion = bf16[3072,256]{1,0:T(8,128)(2,1)S(1)} fusion(f32[3072,256]{1,0:T(8,128)S(1)} %copy-done.46, f32[3072,256]{1,0:T(8,128)} %get-tuple-element.137, bf16[3072,768]{1,0:T(8,128)(2,1)} %bitcast.232, f32[256,768]{1,0:T(8,128)S(1)} %subtract_multiply_fusion.1), kind=kOutput, calls=%fused_computation.6 | convolution fusion | flops 1219166208 | bytes 13369344 | tf_op jit(solution)/shard_map/dot_general | solution.py:691
  206.0 2.4 multiply_reduce_fusion
  209.7 4.8 %concatenate.11 = f32[936,128]{1,0:T(8,128)} concatenate(f32[768,128]{1,0:T(8,128)} %fusion.48, f32[24,128]{1,0:T(8,128)S(1)} %reshape.289, f32[128,128]{1,0:T(8,128)S(1)} %multiply_multiply_fusion.5, f32[14,128]{1,0:T(8,128)S(1)} %multiply_multiply_fusion.6, f32[1,128]{1,0:T(1,128)S(1)} %reshape.290, f32[1,128]{1,0:T(1,128)S(1)} %compare_select_fusion), dimensions={0} | concatenate | bytes 958464 | tf_op jit(solution)/shard_map/concatenate | solution.py:937
  215.4 5.0 %convolution_convert_fusion.1 = bf16[3072,768]{1,0:T(8,128)(2,1)} fusion(bf16[3072,256]{1,0:T(8,128)(2,1)S(1)} %add_convert_fusion, f32[256,768]{1,0:T(8,128)} %copy-done.5, f32[768]{0:T(1024)S(1)} %copy-done.25, f32[768]{0:T(1024)S(1)} %mul.269, f32[256]{0:T(256)S(1)} %copy-done.29, f32[256]{0:T(256)S(1)} %copy-done.27), kind=kOutput, calls=%fused_computation.1 | convolution fusion | flops 1211301888 | bytes 7086080 | tf_op jit(solution)/shard_map/dot_general | solution.py:691
  220.4 3.6 convolution_convert_fusion.2
  224.3 2.5 convolution_convert_fusion.5
  226.8 7.1 %shard_map.301.d_ref = bf16[4,192,256]{2,1,0:T(8,128)(2,1)} custom-call(bf16[4,192,256]{2,1,0:T(8,128)(2,1)} %bitcast.198), custom_call_target="tpu_custom_call" | custom-call | tf_op jit(solution)/shard_map/pallas_call | solution.py:52
  233.9 11.4 %shard_map.302 = (bf16[4,192,256]{2,1,0:T(8,128)(2,1)}, bf16[4,192,256]{2,1,0:T(8,128)(2,1)}, bf16[4,192,256]{2,1,0:T(8,128)(2,1)}) custom-call(bf16[4,576,256]{2,1,0:T(8,128)(2,1)} %shard_map.297.q_ref.k_ref.v_ref, bf16[4,576,256]{2,1,0:T(8,128)(2,1)} %shard_map.297.q_ref.k_ref.v_ref, bf16[4,576,256]{2,1,0:T(8,128)(2,1)} %shard_map.297.q_ref.k_ref.v_ref, ...), custom_call_target="tpu_custom_call" | custom-call | tf_op jit(solution)/shard_map/pallas_call | solution.py:782
  245.3 2.3 pad_maximum_fusion.refs_0_
  247.6 13.5 %shard_map.303 = bf16[4,576,256]{2,1,0:T(8,128)(2,1)} custom-call(bf16[4,576,256]{2,1,0:T(8,128)(2,1)} %pad_maximum_fusion.refs_0_), custom_call_target="tpu_custom_call" | custom-call | tf_op jit(solution)/shard_map/pallas_call | solution.py:52
  261.1 3.5 fusion.8
  264.7 1.5 convolution_convert_fusion.4
  268.4 2.9 convolution_convert_fusion
  271.2 95.0 %shard_map.304 = (bf16[4,256,192]{2,1,0:T(8,128)(2,1)}, bf16[4,256,192]{2,1,0:T(8,128)(2,1)}, bf16[768,384]{1,0:T(8,128)(2,1)}, bf16[768,384]{1,0:T(8,128)(2,1)}...) custom-call(bf16[4,256,192]{2,1,0:T(8,128)(2,1)} %bitcast.195, bf16[4,256,192]{2,1,0:T(8,128)(2,1)} %bitcast.194, ...), custom_call_target="tpu_custom_call" | custom-call | tf_op jit(solution)/shard_map/pallas_call | solution.py:52
  366.2 2.1 copy.59
  368.3 1.6 convert_element_type.134
  382.1 1.5 slice.105
  (194 shorter events, 36.4 us)
Async XLA Ops:
  7.2 177.3 %copy-start = (f32[128,128]{1,0:T(8,128)S(1)}, f32[128,128]{1,0:T(8,128)}, u32[]{:S(2)}) copy-start(f32[128,128]{1,0:T(8,128)} %param.32) | copy-start | bytes 196612
  7.2 8.7 %copy-start.37 = (f32[192]{0:T(256)S(1)}, f32[192]{0:T(256)}, u32[]{:S(2)}) copy-start(f32[192]{0:T(256)} %param.29) | copy-start | bytes 2308
  7.2 8.7 %copy-start.38 = (f32[192]{0:T(256)S(1)}, f32[192]{0:T(256)}, u32[]{:S(2)}) copy-start(f32[192]{0:T(256)} %param.28) | copy-start | bytes 2308
  7.2 8.7 %copy-start.39 = (f32[192]{0:T(256)S(1)}, f32[192]{0:T(256)}, u32[]{:S(2)}) copy-start(f32[192]{0:T(256)} %param.27) | copy-start | bytes 2308
  7.2 8.7 %copy-start.40 = (f32[192]{0:T(256)S(1)}, f32[192]{0:T(256)}, u32[]{:S(2)}) copy-start(f32[192]{0:T(256)} %param.26) | copy-start | bytes 2308
  7.2 368.5 %all-reduce.4.cloned.1.call-start = ((), (), s32[]{:S(2)}) async-start(), calls=%async_computation | async-start | bytes 958464 | tf_op jit(solution)/shard_map/psum | solution.py:948
  8.0 185.0 %copy-start.31 = (f32[2,64]{1,0:T(2,128)}, f32[2,64]{1,0:T(2,128)S(1)}, u32[]{:S(2)}) copy-start(f32[2,64]{1,0:T(2,128)S(1)} %broadcast_multiply_fusion.1) | copy-start | bytes 1540
  115.2 57.1 %copy-start.24 = (f32[768]{0:T(1024)}, f32[768]{0:T(1024)S(1)}, u32[]{:S(2)}) copy-start(f32[768]{0:T(1024)S(1)} %add.89) | copy-start | bytes 9220
  120.6 38.4 %copy-start.10 = (bf16[4,192,768]{2,1,0:T(8,128)(2,1)S(1)}, bf16[4,192,768]{2,1,0:T(8,128)(2,1)}, u32[]{:S(2)}) copy-start(bf16[4,192,768]{2,1,0:T(8,128)(2,1)} %get-tuple-element.41) | copy-start | bytes 3538948
  159.0 13.3 %slice-start.2 = ((s8[4718592]{0:T(1024)(128)(4,1)}), s8[4194304]{0:T(1024)(128)(4,1)S(1)}, s32[]{:S(2)}) async-start(s8[4718592]{0:T(1024)(128)(4,1)} %bitcast.233), calls=%async_computation.3 | async-start | bytes 8388608
  160.8 11.5 %copy-start.5 = (f32[256,768]{1,0:T(8,128)}, f32[256,768]{1,0:T(8,128)S(1)}, u32[]{:S(2)}) copy-start(f32[256,768]{1,0:T(8,128)S(1)} %get-tuple-element.136) | copy-start | bytes 2359300
  160.8 11.5 %copy-start.26 = (f32[256]{0:T(256)}, f32[256]{0:T(256)S(1)}, u32[]{:S(2)}) copy-start(f32[256]{0:T(256)S(1)} %get-tuple-element.134) | copy-start | bytes 3076
  160.9 11.5 %copy-start.28 = (f32[256]{0:T(256)}, f32[256]{0:T(256)S(1)}, u32[]{:S(2)}) copy-start(f32[256]{0:T(256)S(1)} %get-tuple-element.135) | copy-start | bytes 3076
  160.9 11.5 %slice-start.3 = ((s8[4718592]{0:T(1024)(128)(4,1)}), s8[524288]{0:T(1024)(128)(4,1)S(1)}, s32[]{:S(2)}) async-start(s8[4718592]{0:T(1024)(128)(4,1)} %bitcast.233), calls=%async_computation.4 | async-start | bytes 1048576
  172.4 12.2 %copy-start.19 = (f32[128,14]{0,1:T(8,128)S(1)}, f32[128,14]{0,1:T(8,128)}, u32[]{:S(2)}) copy-start(f32[128,14]{0,1:T(8,128)} %param.33) | copy-start | bytes 21508
  172.4 13.6 %copy-start.45 = (s32[4,1]{0,1:T(1,128)S(1)}, s32[4,1]{0,1:T(1,128)}, u32[]{:S(2)}) copy-start(s32[4,1]{0,1:T(1,128)} %param.19) | copy-start | bytes 52
  172.4 21.1 %copy-start.15 = (bf16[4,256,192]{2,1,0:T(8,128)(2,1)S(1)}, bf16[4,256,192]{2,1,0:T(8,128)(2,1)}, u32[]{:S(2)}) copy-start(bf16[4,256,192]{2,1,0:T(8,128)(2,1)} %get-tuple-element.45) | copy-start | bytes 1179652
  174.9 23.6 %copy-start.11 = (bf16[4,192,128]{2,1,0:T(8,128)(2,1)S(1)}, bf16[4,192,128]{2,1,0:T(8,128)(2,1)}, u32[]{:S(2)}) copy-start(bf16[4,192,128]{2,1,0:T(8,128)(2,1)} %get-tuple-element.46) | copy-start | bytes 589828
  175.1 18.4 %copy-start.17 = (f32[2,1,256]{2,1,0:T(1,128)}, f32[2,1,256]{2,1,0:T(1,128)S(1)}, u32[]{:S(2)}) copy-start(f32[2,1,256]{2,1,0:T(1,128)S(1)} %fusion.46) | copy-start | bytes 6148
  193.7 4.3 %copy-start.18 = (f32[2,1,256]{2,1,0:T(1,128)S(1)}, f32[2,1,256]{2,1,0:T(1,128)}, u32[]{:S(2)}) copy-start(f32[2,1,256]{2,1,0:T(1,128)} %copy-done.17) | copy-start | bytes 6148
  193.7 4.7 %copy-start.32 = (f32[2,64]{1,0:T(2,128)S(1)}, f32[2,64]{1,0:T(2,128)}, u32[]{:S(2)}) copy-start(f32[2,64]{1,0:T(2,128)} %copy-done.31) | copy-start | bytes 1540
  193.7 6.3 %copy-start.21 = (f32[256]{0:T(256)S(1)}, f32[256]{0:T(256)}, u32[]{:S(2)}) copy-start(f32[256]{0:T(256)} %copy-done.20) | copy-start | bytes 3076
  193.7 6.3 %copy-start.23 = (f32[256]{0:T(256)S(1)}, f32[256]{0:T(256)}, u32[]{:S(2)}) copy-start(f32[256]{0:T(256)} %copy-done.22) | copy-start | bytes 3076
  200.0 5.8 %slice-start = ((s8[4718592]{0:T(1024)(128)(4,1)}), s8[4194304]{0:T(1024)(128)(4,1)S(1)}, s32[]{:S(2)}) async-start(s8[4718592]{0:T(1024)(128)(4,1)} %bitcast.229), calls=%async_computation.1 | async-start | bytes 8388608
  200.4 5.5 %copy-start.6 = (f32[256,768]{1,0:T(8,128)S(1)}, f32[256,768]{1,0:T(8,128)}, u32[]{:S(2)}) copy-start(f32[256,768]{1,0:T(8,128)} %copy-done.5) | copy-start | bytes 2359300
  200.4 5.5 %copy-start.27 = (f32[256]{0:T(256)S(1)}, f32[256]{0:T(256)}, u32[]{:S(2)}) copy-start(f32[256]{0:T(256)} %copy-done.26) | copy-start | bytes 3076
  200.4 5.5 %copy-start.29 = (f32[256]{0:T(256)S(1)}, f32[256]{0:T(256)}, u32[]{:S(2)}) copy-start(f32[256]{0:T(256)} %copy-done.28) | copy-start | bytes 3076
  200.4 5.6 %slice-start.1 = ((s8[4718592]{0:T(1024)(128)(4,1)}), s8[524288]{0:T(1024)(128)(4,1)S(1)}, s32[]{:S(2)}) async-start(s8[4718592]{0:T(1024)(128)(4,1)} %bitcast.229), calls=%async_computation.2 | async-start | bytes 1048576
  208.4 7.0 %copy-start.25 = (f32[768]{0:T(1024)S(1)}, f32[768]{0:T(1024)}, u32[]{:S(2)}) copy-start(f32[768]{0:T(1024)} %copy-done.24) | copy-start | bytes 9220
  215.4 5.0 %copy-start.4 = (bf16[3072,256]{1,0:T(8,128)(2,1)S(1)}, bf16[3072,256]{1,0:T(8,128)(2,1)}, u32[]{:S(2)}) copy-start(bf16[3072,256]{1,0:T(8,128)(2,1)} %copy-done.3) | copy-start | bytes 4718596
  366.2 6.1 %copy-start.14 = (bf16[768,384]{1,0:T(8,128)(2,1)S(1)}, bf16[768,384]{1,0:T(8,128)(2,1)}, u32[]{:S(2)}) copy-start(bf16[768,384]{1,0:T(8,128)(2,1)} %get-tuple-element.57) | copy-start | bytes 1769476
  372.3 11.3 %copy-start.1 = (f32[128,128]{1,0:T(8,128)S(1)}, f32[128,128]{1,0:T(8,128)}, u32[]{:S(2)}) copy-start(f32[128,128]{1,0:T(8,128)} %param.32) | copy-start | bytes 196612
  (20 other events, 58.2 us)
Sparse Core Ops, SparseCore 0:
  214.6 134.5 all-reduce.3
